TPU v7x, 256 devices: a whole 4x4x8 slice. The times are simulated.
256 devices in a mesh: rows: 32 (over z, x), feat: 8 (over y, core).
Axes of the slice: x: 4, y: 4, z: 8, core: 2. Of those that a mesh axis runs over, the one named last changes fastest.
Arguments:
- tile_values: bfloat16 [8192, 512, 128], P('rows', 'feat'), may hold values from -6 to 6
- tile_blocks: int32 [8192, 512], P('rows', 'feat'), may hold values from 0 to 1023
- tile_counts: int32 [8192, 8], P('rows', 'feat'), may hold values from 1 to 64, as said below
- labels: int32 [8192], P('rows'), may hold values 0 or 1
- owner_rank: int32 [8192], P('rows'), may hold values from 0 to 31, as said below
- weights: float32 [8192, 128], P(('feat', 'rows')), may hold values from -0.09375 to 0.09375
Outputs:
- owned_margins: float32 [8192], P('rows')
- gradient: float32 [8192, 128], P(('feat', 'rows'))
- loss: float32 [], replicated
Inputs may be any that keep to these rules, and one draw needn't show every extreme that they name: `owner_rank`: within each aligned block of 256 examples, every owner is named by exactly 8 examples. `tile_counts`: in every aligned block of 256 examples, each shard's column holds at least one example with exactly 64 used slots.
All inputs are finite; a program needn't handle non-finite values. No bound on the sum of `labels` on one device may be relied on, other than what follows from the above.
Results may differ from a plain program's by a relative error of at most 0.003.
Values may be sent and summed in bfloat16 or wider, within the bound.
A program may use at most 64 MiB of HBM per device.

v0:
```python
import math

import jax
import jax.numpy as jnp
from jax import lax
from jax.sharding import PartitionSpec as P


def sent_to_all(value, axis):
    peers = lax.axis_size(axis)
    return lax.all_to_all(
        jnp.broadcast_to(value[None], (peers, *value.shape)), axis, 0, 0, tiled=True
    )


def joined_along(blocks, dim):
    lengths = list(blocks.shape[1:])
    lengths[dim] *= blocks.shape[0]
    return jnp.moveaxis(blocks, 0, dim).reshape(lengths)


def collect(value, axis, dim):
    blocks = sent_to_all(value, axis)
    return joined_along(blocks, dim)


def taken_together(value, axis):
    return sent_to_all(value, axis).sum(axis=0)


def in_blocks(value, dim, peers):
    lengths = value.shape
    blocks = value.reshape(*lengths[:dim], peers, lengths[dim] // peers, *lengths[dim + 1 :])
    return jnp.moveaxis(blocks, dim, 0)


def sum_at_owner(value, axis, dim):
    blocks = in_blocks(value, dim, lax.axis_size(axis))
    arrived = lax.all_to_all(blocks, axis, split_axis=0, concat_axis=0, tiled=True)
    return arrived.sum(axis=0)


def on_device(tile_values, tile_blocks, tile_counts, labels, owner_rank, weights):
    examples = tile_values.shape[0]
    slot_count = tile_values.shape[1]
    tile_width = tile_values.shape[2]
    peer_count = lax.axis_size("rows")
    per_owner = examples // peer_count
    w_half = weights.astype(jnp.bfloat16)
    weight_table = collect(w_half, "rows", 0)
    owner_hits = (owner_rank[:, None] == jnp.arange(peer_count, dtype=jnp.int32)[None, :]).astype(
        jnp.int32
    )
    earlier = jnp.cumsum(owner_hits, axis=0) - owner_hits
    local_rank = jnp.sum(earlier * owner_hits, axis=1)
    position = owner_rank * per_owner + local_rank
    send_order = (
        jnp.zeros((examples,), jnp.int32).at[position].set(jnp.arange(examples, dtype=jnp.int32))
    )
    counts_here = tile_counts[:, 0]
    live_slot = jnp.arange(slot_count, dtype=jnp.int32)[None, :] < counts_here[:, None]
    picked = weight_table[tile_blocks]
    products = jnp.sum(tile_values.astype(jnp.float32) * picked.astype(jnp.float32), axis=2)
    partial_value = jnp.sum(jnp.where(live_slot, products, jnp.float32(0.0)), axis=1)
    margin = taken_together(partial_value, "feat")
    label_float = labels.astype(jnp.float32)
    residual = jax.nn.sigmoid(margin) - label_float
    loss_terms = jnp.sum(jax.nn.softplus(margin) - label_float * margin)
    loss = taken_together(loss_terms, "rows") / (examples * peer_count)
    resid_half = residual.astype(jnp.bfloat16)
    coefficient = jnp.where(live_slot, resid_half[:, None], jnp.zeros((), jnp.bfloat16))
    total_tiles = examples * slot_count
    block_rows = math.gcd(total_tiles, 1024)
    turn_count = total_tiles // block_rows
    flat_values = tile_values.reshape(turn_count, block_rows, tile_width)
    flat_blocks = tile_blocks.reshape(turn_count, block_rows)
    flat_coefficient = coefficient.reshape(turn_count, block_rows)
    row_count = weights.shape[0] * lax.axis_size("rows")
    candidates = jnp.arange(row_count, dtype=jnp.int32)

    def add_block(running, pieces):
        block_values, block_ids, block_coefficient = pieces
        matches = block_ids[:, None] == candidates[None, :]
        spread = jnp.where(matches, block_coefficient[:, None], jnp.zeros((), jnp.bfloat16))
        update = lax.dot_general(
            spread, block_values, (((0,), (0,)), ((), ())), preferred_element_type=jnp.float32
        )
        return (running + update, None)

    start_sum = jnp.zeros((row_count, tile_width), jnp.float32)
    summed, unused = lax.scan(add_block, start_sum, (flat_values, flat_blocks, flat_coefficient))
    gradient = sum_at_owner(summed, "rows", 0)
    ordered = margin[send_order].reshape(peer_count, per_owner)
    owned_margins = lax.all_to_all(
        ordered, "rows", split_axis=0, concat_axis=0, tiled=True
    ).reshape(examples)
    return (owned_margins, gradient, loss)


def solution(mesh):
    in_specs = (
        P("rows", "feat", None),
        P("rows", "feat"),
        P("rows", "feat"),
        P("rows"),
        P("rows"),
        P(("feat", "rows"), None),
    )
    out_specs = (P("rows"), P(("feat", "rows"), None), P())
    return jax.shard_map(
        on_device, mesh=mesh, in_specs=in_specs, out_specs=out_specs, check_vma=False
    )
```

profile of v0, /device:TPU:1, one launch (start us, length us, event | category | flops | bytes accessed | tf_op | source)
XLA Modules:
  0.0 193.3 jit_solution(1007062431974473650)
XLA Ops:
  0.6 0.7 convert_element_type.23
  1.4 0.7 broadcast_in_dim.71
  2.1 11.9 %all-to-all-start = ((bf16[32,32,128]{2,1,0:T(8,128)(2,1)}), bf16[32,32,128]{2,1,0:T(8,128)(2,1)S(1)}, u32[]{:S(2)}, u32[]{:S(2)}) async-start(bf16[32,32,128]{2,1,0:T(8,128)(2,1)} %broadcast_in_dim.71), calls=%async_computation | async-start | bytes 524288 | tf_op jit(solution)/shard_map/all_to_all | solution.py:11
  13.9 0.9 compare_select_fusion
  14.8 0.7 fusion.19
  15.5 0.6 reduce-window.6
  16.1 0.2 slice_reduce_fusion
  16.3 0.8 fusion.18
  17.1 0.7 compare_select_fusion.4
  17.7 1.4 scatter_custom_fusion
  19.2 0.1 copy.21
  19.3 0.1 reshape.74
  19.4 5.9 %all-to-all-done = bf16[32,32,128]{2,1,0:T(8,128)(2,1)S(1)} async-done(((bf16[32,32,128]{2,1,0:T(8,128)(2,1)}), bf16[32,32,128]{2,1,0:T(8,128)(2,1)S(1)}, u32[]{:S(2)}, u32[]{:S(2)}) %all-to-all-start) | async-done | bytes 262176 | tf_op jit(solution)/shard_map/all_to_all | solution.py:11
  25.3 57.4 %gather_fusion = bf16[16384,128]{1,0:T(8,128)(2,1)} fusion(bf16[1024,128]{1,0:T(8,128)(2,1)S(1)} %bitcast.36, s32[16384]{0:T(1024)S(1)} %broadcast_clamp_fusion), kind=kCustom, calls=%fused_computation | custom fusion | bytes 8454144 | tf_op jit(solution)/shard_map/gather | solution.py:62
  82.6 5.7 %fusion.15 = f32[256,64]{1,0:T(8,128)S(1)} fusion(bf16[256,64,128]{2,1,0:T(8,128)(2,1)} %bitcast.37, bf16[256,64,128]{2,1,0:T(8,128)(2,1)} %param.8), kind=kLoop, calls=%fused_computation.18 | loop fusion | flops 8372224 | bytes 8454144 | tf_op jit(solution)/shard_map/reduce_sum | solution.py:63
  88.4 0.0 copy-done.1
  88.4 0.2 select_reduce_fusion
  88.6 0.6 broadcast_in_dim.74
  89.2 6.9 %all-to-all-start.1 = ((f32[8,1,256]{2,1,0:T(1,128)}), f32[8,1,256]{2,1,0:T(1,128)S(1)}, u32[]{:S(2)}, u32[]{:S(2)}) async-start(f32[8,1,256]{2,1,0:T(1,128)} %broadcast_in_dim.74), calls=%async_computation.1 | async-start | bytes 16384 | tf_op jit(solution)/shard_map/all_to_all | solution.py:11
  96.1 0.0 copy-done
  96.1 0.1 copy.26
  96.2 0.1 reshape.69
  96.3 0.5 broadcast.73
  96.8 0.7 reduce.13
  97.5 0.1 lt.56
  97.6 0.1 lt.57
  97.7 0.1 lt.58
  97.8 0.1 lt.54
  97.9 2.9 %all-to-all-done.1 = f32[8,1,256]{2,1,0:T(1,128)S(1)} async-done(((f32[8,1,256]{2,1,0:T(1,128)}), f32[8,1,256]{2,1,0:T(1,128)S(1)}, u32[]{:S(2)}, u32[]{:S(2)}) %all-to-all-start.1) | async-done | bytes 8224 | tf_op jit(solution)/shard_map/all_to_all | solution.py:11
  100.8 0.6 fusion.21
  101.4 0.1 broadcast_in_dim.78
  101.5 0.1 broadcast_in_dim.79
  101.6 0.1 broadcast_in_dim.80
  101.7 1.3 broadcast_in_dim.82
  102.9 3.9 %all-to-all-start.4 = ((f32[32,1,1]{2,1,0:T(1,128)}), f32[32,1,1]{2,1,0:T(1,128)S(1)}, u32[]{:S(2)}, u32[]{:S(2)}) async-start(f32[32,1,1]{2,1,0:T(1,128)} %broadcast_in_dim.82), calls=%async_computation.4 | async-start | bytes 32768 | tf_op jit(solution)/shard_map/all_to_all | solution.py:11
  106.8 1.9 %gather_fusion.1 = f32[256]{0:T(256)S(1)} fusion(f32[256]{0:T(256)S(1)} %reduce_sum.65, s32[1024]{0:T(1024)S(1)} %pad_clamp_fusion), kind=kCustom, calls=%fused_computation.1 | custom fusion | bytes 3072 | tf_op jit(solution)/shard_map/gather | solution.py:93
  108.8 0.7 all_to_all.22
  109.5 5.9 %all-to-all-done.4 = f32[32,1,1]{2,1,0:T(1,128)S(1)} async-done(((f32[32,1,1]{2,1,0:T(1,128)}), f32[32,1,1]{2,1,0:T(1,128)S(1)}, u32[]{:S(2)}, u32[]{:S(2)}) %all-to-all-start.4) | async-done | bytes 160 | tf_op jit(solution)/shard_map/all_to_all | solution.py:11
  115.4 3.8 %all-to-all-start.2 = ((f32[32,1,8]{2,1,0:T(1,128)}), f32[32,1,8]{2,1,0:T(1,128)S(1)}, u32[]{:S(2)}, u32[]{:S(2)}) async-start(f32[32,1,8]{2,1,0:T(1,128)} %bitcast.5), calls=%async_computation.2 | async-start | bytes 32768 | tf_op jit(solution)/shard_map/all_to_all | solution.py:94
  119.3 48.5 %while.11 = (s32[]{:T(128)}, f32[1024,128]{1,0:T(8,128)}, s32[16,1024]{1,0:T(8,128)S(1)}, bf16[16,1024]{1,0:T(8,128)(2,1)S(1)}, bf16[16,1024,128]{2,1,0:T(8,128)(2,1)}, /*index=5*/s32[]{:T(128)}, s32[]{:T(128)}) while((s32[]{:T(128)}, f32[1024,128]{1,0:T(8,128)}, s32[16,1024]{1,0:T(8,128)S(1)}, bf16[16,1024]{1,0:T(8,128)(2,1)S(1)}, ...), condition=%wide.region_8.9_spmd.clone, body=%wide.region_7.8_spmd.clone.sunk | while | flops 270794752 | bytes 1329259 | solution.py:91
  119.3 2.8 %fusion.30 = f32[1024,128]{1,0:T(8,128)} fusion(s32[1024]{0:T(1024)S(1)} %bitcast.39, bf16[1024]{0:T(1024)(128)(2,1)S(1)} %dynamic-slice_reduce_fusion.2, f32[1024,128]{1,0:T(8,128)} %get-tuple-element.107, bf16[16,1024,128]{2,1,0:T(8,128)(2,1)} %get-tuple-element.117, s32[]{:T(128)S(6)} %copy.35, pred[]{:T(512)S(6)} %compare.3), kind=kOutput, calls=%fused_computation.8.clone.1 | convolution fusion | flops 270794752 | bytes 1316869 | tf_op jit(solution)/shard_map/while/body/eval_jaxpr/dot_general | solution.py:85
  122.2 3.0 %fusion.30 = f32[1024,128]{1,0:T(8,128)} fusion(s32[1024]{0:T(1024)S(1)} %bitcast.39, bf16[1024]{0:T(1024)(128)(2,1)S(1)} %dynamic-slice_reduce_fusion.2, f32[1024,128]{1,0:T(8,128)} %get-tuple-element.107, bf16[16,1024,128]{2,1,0:T(8,128)(2,1)} %get-tuple-element.117, s32[]{:T(128)S(6)} %copy.35, pred[]{:T(512)S(6)} %compare.3), kind=kOutput, calls=%fused_computation.8.clone.1 | convolution fusion | flops 270794752 | bytes 1316869 | tf_op jit(solution)/shard_map/while/body/eval_jaxpr/dot_general | solution.py:85
  125.2 3.0 %fusion.30 = f32[1024,128]{1,0:T(8,128)} fusion(s32[1024]{0:T(1024)S(1)} %bitcast.39, bf16[1024]{0:T(1024)(128)(2,1)S(1)} %dynamic-slice_reduce_fusion.2, f32[1024,128]{1,0:T(8,128)} %get-tuple-element.107, bf16[16,1024,128]{2,1,0:T(8,128)(2,1)} %get-tuple-element.117, s32[]{:T(128)S(6)} %copy.35, pred[]{:T(512)S(6)} %compare.3), kind=kOutput, calls=%fused_computation.8.clone.1 | convolution fusion | flops 270794752 | bytes 1316869 | tf_op jit(solution)/shard_map/while/body/eval_jaxpr/dot_general | solution.py:85
  128.3 3.0 %fusion.30 = f32[1024,128]{1,0:T(8,128)} fusion(s32[1024]{0:T(1024)S(1)} %bitcast.39, bf16[1024]{0:T(1024)(128)(2,1)S(1)} %dynamic-slice_reduce_fusion.2, f32[1024,128]{1,0:T(8,128)} %get-tuple-element.107, bf16[16,1024,128]{2,1,0:T(8,128)(2,1)} %get-tuple-element.117, s32[]{:T(128)S(6)} %copy.35, pred[]{:T(512)S(6)} %compare.3), kind=kOutput, calls=%fused_computation.8.clone.1 | convolution fusion | flops 270794752 | bytes 1316869 | tf_op jit(solution)/shard_map/while/body/eval_jaxpr/dot_general | solution.py:85
  131.3 3.0 %fusion.30 = f32[1024,128]{1,0:T(8,128)} fusion(s32[1024]{0:T(1024)S(1)} %bitcast.39, bf16[1024]{0:T(1024)(128)(2,1)S(1)} %dynamic-slice_reduce_fusion.2, f32[1024,128]{1,0:T(8,128)} %get-tuple-element.107, bf16[16,1024,128]{2,1,0:T(8,128)(2,1)} %get-tuple-element.117, s32[]{:T(128)S(6)} %copy.35, pred[]{:T(512)S(6)} %compare.3), kind=kOutput, calls=%fused_computation.8.clone.1 | convolution fusion | flops 270794752 | bytes 1316869 | tf_op jit(solution)/shard_map/while/body/eval_jaxpr/dot_general | solution.py:85
  134.4 3.0 %fusion.30 = f32[1024,128]{1,0:T(8,128)} fusion(s32[1024]{0:T(1024)S(1)} %bitcast.39, bf16[1024]{0:T(1024)(128)(2,1)S(1)} %dynamic-slice_reduce_fusion.2, f32[1024,128]{1,0:T(8,128)} %get-tuple-element.107, bf16[16,1024,128]{2,1,0:T(8,128)(2,1)} %get-tuple-element.117, s32[]{:T(128)S(6)} %copy.35, pred[]{:T(512)S(6)} %compare.3), kind=kOutput, calls=%fused_computation.8.clone.1 | convolution fusion | flops 270794752 | bytes 1316869 | tf_op jit(solution)/shard_map/while/body/eval_jaxpr/dot_general | solution.py:85
  137.4 3.0 %fusion.30 = f32[1024,128]{1,0:T(8,128)} fusion(s32[1024]{0:T(1024)S(1)} %bitcast.39, bf16[1024]{0:T(1024)(128)(2,1)S(1)} %dynamic-slice_reduce_fusion.2, f32[1024,128]{1,0:T(8,128)} %get-tuple-element.107, bf16[16,1024,128]{2,1,0:T(8,128)(2,1)} %get-tuple-element.117, s32[]{:T(128)S(6)} %copy.35, pred[]{:T(512)S(6)} %compare.3), kind=kOutput, calls=%fused_computation.8.clone.1 | convolution fusion | flops 270794752 | bytes 1316869 | tf_op jit(solution)/shard_map/while/body/eval_jaxpr/dot_general | solution.py:85
  140.4 3.0 %fusion.30 = f32[1024,128]{1,0:T(8,128)} fusion(s32[1024]{0:T(1024)S(1)} %bitcast.39, bf16[1024]{0:T(1024)(128)(2,1)S(1)} %dynamic-slice_reduce_fusion.2, f32[1024,128]{1,0:T(8,128)} %get-tuple-element.107, bf16[16,1024,128]{2,1,0:T(8,128)(2,1)} %get-tuple-element.117, s32[]{:T(128)S(6)} %copy.35, pred[]{:T(512)S(6)} %compare.3), kind=kOutput, calls=%fused_computation.8.clone.1 | convolution fusion | flops 270794752 | bytes 1316869 | tf_op jit(solution)/shard_map/while/body/eval_jaxpr/dot_general | solution.py:85
  143.5 3.0 %fusion.30 = f32[1024,128]{1,0:T(8,128)} fusion(s32[1024]{0:T(1024)S(1)} %bitcast.39, bf16[1024]{0:T(1024)(128)(2,1)S(1)} %dynamic-slice_reduce_fusion.2, f32[1024,128]{1,0:T(8,128)} %get-tuple-element.107, bf16[16,1024,128]{2,1,0:T(8,128)(2,1)} %get-tuple-element.117, s32[]{:T(128)S(6)} %copy.35, pred[]{:T(512)S(6)} %compare.3), kind=kOutput, calls=%fused_computation.8.clone.1 | convolution fusion | flops 270794752 | bytes 1316869 | tf_op jit(solution)/shard_map/while/body/eval_jaxpr/dot_general | solution.py:85
  146.5 3.0 %fusion.30 = f32[1024,128]{1,0:T(8,128)} fusion(s32[1024]{0:T(1024)S(1)} %bitcast.39, bf16[1024]{0:T(1024)(128)(2,1)S(1)} %dynamic-slice_reduce_fusion.2, f32[1024,128]{1,0:T(8,128)} %get-tuple-element.107, bf16[16,1024,128]{2,1,0:T(8,128)(2,1)} %get-tuple-element.117, s32[]{:T(128)S(6)} %copy.35, pred[]{:T(512)S(6)} %compare.3), kind=kOutput, calls=%fused_computation.8.clone.1 | convolution fusion | flops 270794752 | bytes 1316869 | tf_op jit(solution)/shard_map/while/body/eval_jaxpr/dot_general | solution.py:85
  149.6 3.0 %fusion.30 = f32[1024,128]{1,0:T(8,128)} fusion(s32[1024]{0:T(1024)S(1)} %bitcast.39, bf16[1024]{0:T(1024)(128)(2,1)S(1)} %dynamic-slice_reduce_fusion.2, f32[1024,128]{1,0:T(8,128)} %get-tuple-element.107, bf16[16,1024,128]{2,1,0:T(8,128)(2,1)} %get-tuple-element.117, s32[]{:T(128)S(6)} %copy.35, pred[]{:T(512)S(6)} %compare.3), kind=kOutput, calls=%fused_computation.8.clone.1 | convolution fusion | flops 270794752 | bytes 1316869 | tf_op jit(solution)/shard_map/while/body/eval_jaxpr/dot_general | solution.py:85
  152.6 3.0 %fusion.30 = f32[1024,128]{1,0:T(8,128)} fusion(s32[1024]{0:T(1024)S(1)} %bitcast.39, bf16[1024]{0:T(1024)(128)(2,1)S(1)} %dynamic-slice_reduce_fusion.2, f32[1024,128]{1,0:T(8,128)} %get-tuple-element.107, bf16[16,1024,128]{2,1,0:T(8,128)(2,1)} %get-tuple-element.117, s32[]{:T(128)S(6)} %copy.35, pred[]{:T(512)S(6)} %compare.3), kind=kOutput, calls=%fused_computation.8.clone.1 | convolution fusion | flops 270794752 | bytes 1316869 | tf_op jit(solution)/shard_map/while/body/eval_jaxpr/dot_general | solution.py:85
  155.6 3.0 %fusion.30 = f32[1024,128]{1,0:T(8,128)} fusion(s32[1024]{0:T(1024)S(1)} %bitcast.39, bf16[1024]{0:T(1024)(128)(2,1)S(1)} %dynamic-slice_reduce_fusion.2, f32[1024,128]{1,0:T(8,128)} %get-tuple-element.107, bf16[16,1024,128]{2,1,0:T(8,128)(2,1)} %get-tuple-element.117, s32[]{:T(128)S(6)} %copy.35, pred[]{:T(512)S(6)} %compare.3), kind=kOutput, calls=%fused_computation.8.clone.1 | convolution fusion | flops 270794752 | bytes 1316869 | tf_op jit(solution)/shard_map/while/body/eval_jaxpr/dot_general | solution.py:85
  158.7 3.0 %fusion.30 = f32[1024,128]{1,0:T(8,128)} fusion(s32[1024]{0:T(1024)S(1)} %bitcast.39, bf16[1024]{0:T(1024)(128)(2,1)S(1)} %dynamic-slice_reduce_fusion.2, f32[1024,128]{1,0:T(8,128)} %get-tuple-element.107, bf16[16,1024,128]{2,1,0:T(8,128)(2,1)} %get-tuple-element.117, s32[]{:T(128)S(6)} %copy.35, pred[]{:T(512)S(6)} %compare.3), kind=kOutput, calls=%fused_computation.8.clone.1 | convolution fusion | flops 270794752 | bytes 1316869 | tf_op jit(solution)/shard_map/while/body/eval_jaxpr/dot_general | solution.py:85
  161.7 3.0 %fusion.30 = f32[1024,128]{1,0:T(8,128)} fusion(s32[1024]{0:T(1024)S(1)} %bitcast.39, bf16[1024]{0:T(1024)(128)(2,1)S(1)} %dynamic-slice_reduce_fusion.2, f32[1024,128]{1,0:T(8,128)} %get-tuple-element.107, bf16[16,1024,128]{2,1,0:T(8,128)(2,1)} %get-tuple-element.117, s32[]{:T(128)S(6)} %copy.35, pred[]{:T(512)S(6)} %compare.3), kind=kOutput, calls=%fused_computation.8.clone.1 | convolution fusion | flops 270794752 | bytes 1316869 | tf_op jit(solution)/shard_map/while/body/eval_jaxpr/dot_general | solution.py:85
  164.8 3.0 %fusion.30 = f32[1024,128]{1,0:T(8,128)} fusion(s32[1024]{0:T(1024)S(1)} %bitcast.39, bf16[1024]{0:T(1024)(128)(2,1)S(1)} %dynamic-slice_reduce_fusion.2, f32[1024,128]{1,0:T(8,128)} %get-tuple-element.107, bf16[16,1024,128]{2,1,0:T(8,128)(2,1)} %get-tuple-element.117, s32[]{:T(128)S(6)} %copy.35, pred[]{:T(512)S(6)} %compare.3), kind=kOutput, calls=%fused_computation.8.clone.1 | convolution fusion | flops 270794752 | bytes 1316869 | tf_op jit(solution)/shard_map/while/body/eval_jaxpr/dot_general | solution.py:85
  167.7 0.0 all-to-all-done.2
  167.7 9.2 %all-to-all-start.3 = ((f32[32,32,128]{2,1,0:T(8,128)}), f32[32,32,128]{2,1,0:T(8,128)S(1)}, u32[]{:S(2)}, u32[]{:S(2)}) async-start(f32[32,32,128]{2,1,0:T(8,128)} %bitcast.7), calls=%async_computation.3 | async-start | bytes 1048576 | tf_op jit(solution)/shard_map/all_to_all | solution.py:39
  177.0 0.6 reduce_sum.69
  178.3 0.5 broadcast.72
  178.8 0.7 reduce.12
  179.5 0.7 reshape.68
  180.1 11.4 %all-to-all-done.3 = f32[32,32,128]{2,1,0:T(8,128)S(1)} async-done(((f32[32,32,128]{2,1,0:T(8,128)}), f32[32,32,128]{2,1,0:T(8,128)S(1)}, u32[]{:S(2)}, u32[]{:S(2)}) %all-to-all-start.3) | async-done | bytes 524320 | tf_op jit(solution)/shard_map/all_to_all | solution.py:39
  191.5 0.6 reduce_sum.67
  (46 shorter events, 0.7 us)
Async XLA Ops:
  2.1 23.2 %all-to-all-start = ((bf16[32,32,128]{2,1,0:T(8,128)(2,1)}), bf16[32,32,128]{2,1,0:T(8,128)(2,1)S(1)}, u32[]{:S(2)}, u32[]{:S(2)}) async-start(bf16[32,32,128]{2,1,0:T(8,128)(2,1)} %broadcast_in_dim.71), calls=%async_computation | async-start | bytes 524288 | tf_op jit(solution)/shard_map/all_to_all | solution.py:11
  82.6 5.8 %copy-start.1 = (s32[256,1]{0,1:T(1,128)S(1)}, s32[256,1]{0,1:T(1,128)}, u32[]{:S(2)}) copy-start(s32[256,1]{0,1:T(1,128)} %param.10) | copy-start | bytes 3076
  82.6 13.5 %copy-start = (s32[256,64]{0,1:T(8,128)S(1)}, s32[256,64]{0,1:T(8,128)}, u32[]{:S(2)}) copy-start(s32[256,64]{0,1:T(8,128)} %param.9) | copy-start | bytes 196612
  82.6 18.1 %copy-start.2 = (s32[256]{0:T(256)S(1)}, s32[256]{0:T(256)}, u32[]{:S(2)}) copy-start(s32[256]{0:T(256)} %param.11) | copy-start | bytes 3076
  89.2 11.5 %all-to-all-start.1 = ((f32[8,1,256]{2,1,0:T(1,128)}), f32[8,1,256]{2,1,0:T(1,128)S(1)}, u32[]{:S(2)}, u32[]{:S(2)}) async-start(f32[8,1,256]{2,1,0:T(1,128)} %broadcast_in_dim.74), calls=%async_computation.1 | async-start | bytes 16384 | tf_op jit(solution)/shard_map/all_to_all | solution.py:11
  102.9 12.5 %all-to-all-start.4 = ((f32[32,1,1]{2,1,0:T(1,128)}), f32[32,1,1]{2,1,0:T(1,128)S(1)}, u32[]{:S(2)}, u32[]{:S(2)}) async-start(f32[32,1,1]{2,1,0:T(1,128)} %broadcast_in_dim.82), calls=%async_computation.4 | async-start | bytes 32768 | tf_op jit(solution)/shard_map/all_to_all | solution.py:11
  115.4 52.3 %all-to-all-start.2 = ((f32[32,1,8]{2,1,0:T(1,128)}), f32[32,1,8]{2,1,0:T(1,128)S(1)}, u32[]{:S(2)}, u32[]{:S(2)}) async-start(f32[32,1,8]{2,1,0:T(1,128)} %bitcast.5), calls=%async_computation.2 | async-start | bytes 32768 | tf_op jit(solution)/shard_map/all_to_all | solution.py:94
  167.7 23.8 %all-to-all-start.3 = ((f32[32,32,128]{2,1,0:T(8,128)}), f32[32,32,128]{2,1,0:T(8,128)S(1)}, u32[]{:S(2)}, u32[]{:S(2)}) async-start(f32[32,32,128]{2,1,0:T(8,128)} %bitcast.7), calls=%async_computation.3 | async-start | bytes 1048576 | tf_op jit(solution)/shard_map/all_to_all | solution.py:39
where the time goes:
time: 196 us; the launch traced here: 193 us
  local copies, waits for them, and re-layouts  67.5 us (34%)
  matrix products  47.7 us (24%)
  starting transfers between devices  35.7 us (18%)
  waiting for transfers between devices  26.1 us (13%)
  other arithmetic  13.6 us (7%)
  between operations  2.58 us (1%)
    gather x1, local copies, waits for them, and re-layouts, on_device(): picked = weight_table[tile_blocks]  57.4 us
    dot_general x16, matrix products, add_block(): lax.dot_general(spread, block_values, (((0,), (0,)), ((), ())), preferred...  47.7 us
    all_to_all x3, starting transfers between devices, sent_to_all(): lax.all_to_all(jnp.broadcast_to(value[None], (peers, *value.shape)), axis...  22.6 us
    all_to_all x3, waiting for transfers between devices, sent_to_all(): lax.all_to_all(jnp.broadcast_to(value[None], (peers, *value.shape)), axis...  14.7 us
    all_to_all x1, waiting for transfers between devices, sum_at_owner(): lax.all_to_all(blocks, axis, split_axis=0, concat_axis=0, tiled=True)  11.4 us
    all_to_all x1, starting transfers between devices, sum_at_owner(): lax.all_to_all(blocks, axis, split_axis=0, concat_axis=0, tiled=True)  9.21 us
    reduce_sum x1, other arithmetic, on_device(): jnp.sum(tile_values.astype(jnp.float32) * picked.astype(jnp.float32), axi...  5.74 us
  transfers between devices with their start and end apart: 5, of which 4 were waited for; matrix products, arithmetic and copies ran while one was open for 31% of the time, Pallas kernels for 0%

commit v1 on v0

v1 whole, which is shorter than its diff:
```python
import jax
import jax.numpy as jnp
from jax import lax
from jax.experimental import pallas as pl
from jax.experimental.pallas import tpu as pltpu
from jax.sharding import PartitionSpec as P

MESH = pl.DeviceIdType.MESH
NZ, NX = 8, 4
N_ROWS = NZ * NX
N_FEAT = 8
BF = jnp.bfloat16
F32 = jnp.float32
I16 = jnp.int16
I32 = jnp.int32
PAIRS = 128
GROUP = 8
VCHUNKS = 8


def iota(shape, dim, dtype=I32):
    return lax.broadcasted_iota(I32, shape, dim).astype(dtype)


def body(
    values_hbm, blocks_ref, counts_ref, labels_ref, owner_ref, w_ref,
    own_out, grad_out, loss_out,
    vbuf, vx, onehot, acc, wtab, wcat, cct, qrow, coef, rankhot,
    mbuf, sbuf, rbuf, xrow, gacc, gsend, grecv,
    vsem, zs, zr, xs, xr, ms, mr, os_, or_, gs, gr,
):
    r = lax.axis_index("rows")
    f = lax.axis_index("feat")
    z = r // NX
    x = r % NX

    def row_at(dz, dx):
        return ((z + dz) % NZ) * NX + (x + dx) % NX

    def vcopy(i):
        n = 2 * PAIRS // VCHUNKS
        part = pl.ds(i * n, n)
        return pltpu.make_async_copy(values_hbm.at[part], vbuf.at[part], vsem.at[i])

    for i in range(VCHUNKS // 2):
        vcopy(i).start()
        vcopy(i + VCHUNKS // 2).start()
    wtab[2, 0] = w_ref[...].astype(BF)

    barrier = pltpu.get_barrier_semaphore()
    for dz in range(1, NZ):
        pl.semaphore_signal(barrier, inc=1, device_id={"rows": row_at(dz, 0)}, device_id_type=MESH)
    for dx in range(1, NX):
        pl.semaphore_signal(barrier, inc=1, device_id={"rows": row_at(0, dx)}, device_id_type=MESH)
    for df in range(1, N_FEAT):
        pl.semaphore_signal(barrier, inc=1, device_id={"feat": (f + df) % N_FEAT}, device_id_type=MESH)

    blocks = blocks_ref[...]
    dz2 = (lax.shift_right_logical(blocks, 7) - z + (2 + NZ)) & (NZ - 1)
    dxb = (lax.shift_right_logical(blocks, 5) - x + NX) & (NX - 1)
    stage = lax.shift_right_logical(dz2, 2)
    half = lax.shift_right_logical(dz2, 1) & 1
    code = half * 512 + stage * 256 + (dz2 & 1) * 128 + dxb * 32 + (blocks & 31)
    code = jnp.where(iota(blocks.shape, 1) < counts_ref[...], code, -1)
    pair_code = jnp.concatenate([code[:PAIRS], code[PAIRS:]], axis=1)
    qrow[...] = pair_code & 511
    cct[...] = pair_code.T

    pl.semaphore_wait(barrier, NZ - 1 + NX - 1 + N_FEAT - 1)

    def zcopy(dz):
        slot = (dz + 2) % NZ
        return pltpu.make_async_remote_copy(
            wtab.at[2, 0], wtab.at[slot, 0], zs.at[dz - 1], zr.at[dz - 1],
            device_id={"rows": row_at(NZ - dz, 0)}, device_id_type=MESH)

    def xcopy(slot, dx):
        return pltpu.make_async_remote_copy(
            wtab.at[slot, 0], wtab.at[slot, dx], xs.at[slot, dx - 1], xr.at[slot, dx - 1],
            device_id={"rows": row_at(0, NX - dx)}, device_id_type=MESH)

    for dz in (4, 3, 5, 2, 6, 1, 7):
        zcopy(dz).start()
    for dx in (2, 1, 3):
        xcopy(2, dx).start()

    for h in range(2):
        mine = jnp.broadcast_to(owner_ref[pl.ds(h, 1), :], (PAIRS, PAIRS)).T
        rank = jnp.zeros((PAIRS, 1), F32)
        for g in range(2):
            same = (mine == owner_ref[pl.ds(g, 1), :]) & (
                iota((PAIRS, PAIRS), 1) + g * PAIRS < iota((PAIRS, PAIRS), 0) + h * PAIRS)
            rank = rank + jnp.sum(jnp.where(same, 1.0, 0.0), axis=1, keepdims=True)
        lane = (iota((PAIRS, PAIRS), 1) - 8 * (r % 16)).astype(F32)
        rankhot[pl.ds(h * PAIRS, PAIRS), :] = jnp.where(rank == lane, 1.0, 0.0).astype(BF)

    def build(i, _):
        codes = cct[...]
        for u in range(GROUP):
            k = i * GROUP + u
            wide = jnp.broadcast_to(codes[:, u:u + 1], (PAIRS, PAIRS))
            c16 = wide.astype(I16)
            q16 = (wide & 511).astype(I16)
            rows = pl.ds(pl.multiple_of(k * PAIRS, PAIRS), PAIRS)
            for t in range(4):
                hit = q16 == iota((PAIRS, PAIRS), 1, I16) + jnp.int16(128 * t)
                onehot[rows, t * 128:(t + 1) * 128] = jnp.where(hit, jnp.ones((), BF), jnp.zeros((), BF))
            v = jnp.concatenate([vbuf[k], vbuf[k + PAIRS]], axis=0)
            zero = jnp.zeros((), BF)
            high = c16 >= jnp.int16(512)
            low = c16 >= jnp.int16(0)
            v1 = jnp.where(high, v, zero)
            vx[rows, 0:128] = jnp.where(low, v - v1, zero)
            vx[rows, 128:256] = v1
        cct[...] = pltpu.roll(codes, PAIRS - GROUP, 1)
        return 0

    steps = PAIRS // GROUP
    quarter = steps // 4
    for part, arrivals in enumerate(((1, 7), (2, 6), (3, 5), (4,))):
        vcopy(part).wait()
        vcopy(part + VCHUNKS // 2).wait()
        lax.fori_loop(part * quarter, (part + 1) * quarter, build, 0)
        for dz in arrivals:
            zcopy(dz).wait_recv()
            for dx in (2, 1, 3):
                xcopy((dz + 2) % NZ, dx).start()

    for s in range(2):
        for slot in range(4 * s, 4 * s + 4):
            for dx in range(1, NX):
                xcopy(slot, dx).wait_recv()
        for h in range(2):
            for j in range(2):
                wcat[s, j * 128:(j + 1) * 128, h * 128:(h + 1) * 128] = (
                    wtab[4 * s + 2 * h + j].reshape(128, 128))

        def forward(i, _, s=s):
            rows = pl.ds(pl.multiple_of(i * (GROUP * PAIRS), GROUP * PAIRS), GROUP * PAIRS)
            out = jnp.dot(onehot[rows, s * 256:(s + 1) * 256], wcat[s], preferred_element_type=F32)
            prod = out * vx[rows, :].astype(F32)
            prod = prod[:, :128] + prod[:, 128:]
            prod = prod.reshape(GROUP, 2, 8, 8, 128).sum(axis=2)
            ks = pl.ds(i * GROUP, GROUP)
            if s == 0:
                acc[ks] = prod
            else:
                acc[ks] = acc[ks] + prod
            return 0

        lax.fori_loop(0, steps, forward, 0)

    for h in range(2):
        rows_sum = acc[:, h].sum(axis=1)
        mbuf[f, pl.ds(h, 1), :] = jnp.sum(rows_sum.T, axis=0, keepdims=True)

    def mcopy(df):
        return pltpu.make_async_remote_copy(
            mbuf.at[f], mbuf.at[f], ms.at[df - 1], mr.at[df - 1],
            device_id={"feat": (f + df) % N_FEAT}, device_id_type=MESH)

    def mcopy_in(df):
        src = (f + N_FEAT - df) % N_FEAT
        return pltpu.make_async_remote_copy(
            mbuf.at[src], mbuf.at[src], ms.at[df - 1], mr.at[df - 1],
            device_id={"feat": (f + df) % N_FEAT}, device_id_type=MESH)

    for df in (4, 3, 5, 2, 6, 1, 7):
        mcopy(df).start()
    for df in range(1, N_FEAT):
        mcopy_in(df).wait_recv()
    margin = mbuf[0]
    for i in range(1, N_FEAT):
        margin = margin + mbuf[i]
    label = labels_ref[...].astype(F32)
    residual = 1.0 / (1.0 + jnp.exp(-margin)) - label
    resid_half = residual.astype(BF).astype(F32)
    spread = [jnp.broadcast_to(resid_half[h:h + 1, :], (PAIRS, PAIRS)).T for h in range(2)]
    coef[...] = jnp.where(iota((PAIRS, PAIRS), 1) < 64, spread[0], spread[1])

    def gcopy(slot, dx):
        dz = (slot + NZ - 2) % NZ
        return pltpu.make_async_remote_copy(
            gsend.at[slot, dx], grecv.at[slot, dx], gs.at[slot, dx], gr.at[slot, dx],
            device_id={"rows": row_at(dz, dx)}, device_id_type=MESH)

    def gradient_half(s):
        gacc[...] = jnp.zeros(gacc.shape, F32)

        def step(i, _):
            total = None
            for t in range(GROUP // 2):
                left = []
                for u in range(2):
                    k = i * GROUP + 2 * t + u
                    q16 = jnp.broadcast_to(qrow[pl.ds(k, 1), :], (16, PAIRS)).astype(I16)
                    c16 = jnp.broadcast_to(coef[pl.ds(k, 1), :], (16, PAIRS)).astype(BF)
                    q16 = jnp.concatenate([q16] * 16, axis=0)
                    c16 = jnp.concatenate([c16] * 16, axis=0)
                    hit = q16 == iota((256, PAIRS), 0, I16) + jnp.int16(256 * s)
                    left.append(jnp.where(hit, c16, jnp.zeros((), BF)))
                start = pl.multiple_of((i * GROUP + 2 * t) * PAIRS, 2 * PAIRS)
                d = jnp.dot(jnp.concatenate(left, axis=1), vx[pl.ds(start, 2 * PAIRS), :],
                            preferred_element_type=F32)
                total = d if total is None else total + d
            gacc[...] += total
            return 0

        lax.fori_loop(0, steps, step, 0)

    def send_half(s):
        for j in range(2):
            for h in range(2):
                slot = 4 * s + 2 * h + j
                for dx in range(NX):
                    lo = j * 128 + dx * 32
                    block = gacc[lo:lo + 32, h * 128:(h + 1) * 128]
                    if slot == 2 and dx == 0:
                        grad_out[...] = block
                    else:
                        gsend[slot, dx] = block.astype(BF)
        for slot in ((6, 5, 7, 4) if s else (0, 3, 1, 2)):
            for dx in (2, 1, 3, 0):
                if slot != 2 or dx != 0:
                    gcopy(slot, dx).start()

    gradient_half(1)
    send_half(1)

    loss_terms = jnp.maximum(margin, 0.0) + jnp.log1p(jnp.exp(-jnp.abs(margin))) - label * margin
    loss_here = jnp.sum(jnp.sum(loss_terms, axis=1, keepdims=True), axis=0, keepdims=True)
    ordered = jnp.zeros((N_ROWS, 128), F32)
    left = margin
    for _ in range(3):
        piece = left.astype(BF).astype(F32)
        left = left - piece
        pick = jnp.concatenate(
            [jnp.where(owner_ref[pl.ds(h, 1), :] == iota((N_ROWS, 128), 0), piece[h:h + 1, :], 0.0)
             for h in range(2)], axis=1).astype(BF)
        ordered = ordered + jnp.dot(pick, rankhot[...], preferred_element_type=F32)
    lane_group = lax.shift_right_logical(iota((N_ROWS, 128), 1), 3)
    xrow[...] = jnp.where(lane_group == (r + 1) % 16, loss_here, ordered)
    for d in range(N_ROWS):
        sbuf[d] = xrow[d:d + 1, :]
    rbuf[r] = xrow[pl.ds(r, 1), :]

    def ocopy(i):
        to = row_at(i // NX, i % NX)
        return pltpu.make_async_remote_copy(
            sbuf.at[to], rbuf.at[r], os_.at[i - 1], or_.at[i - 1],
            device_id={"rows": to}, device_id_type=MESH)

    def ocopy_in(i):
        src = row_at(NZ - i // NX, NX - i % NX)
        return pltpu.make_async_remote_copy(
            sbuf.at[src], rbuf.at[src], os_.at[i - 1], or_.at[i - 1],
            device_id={"rows": src}, device_id_type=MESH)

    for i in range(1, N_ROWS):
        ocopy(i).start()

    gradient_half(0)
    send_half(0)

    for i in range(1, N_ROWS):
        ocopy_in(i).wait_recv()
    group1 = lax.shift_right_logical(iota((1, 128), 1), 3)
    loss_sum = jnp.zeros((1, 128), F32)
    for h in range(2):
        mine = jnp.zeros((1, 128), F32)
        for g in range(16):
            row = rbuf[h * 16 + g]
            mine = mine + jnp.where(group1 == g, row, 0.0)
            loss_sum = loss_sum + jnp.where(group1 == (g + 1) % 16, row, 0.0)
        own_out[pl.ds(h, 1), :] = mine
    loss_total = jnp.sum(loss_sum, axis=1, keepdims=True) * (1.0 / (8.0 * 8192.0))
    loss_out[...] = jnp.broadcast_to(loss_total, (1, 128))

    total = grad_out[...]
    for slot in (1, 3, 0, 4, 7, 5, 6, 2):
        for dx in range(NX):
            if slot != 2 or dx != 0:
                gcopy(slot, dx).wait_recv()
                total = total + grecv[slot, dx].astype(F32)
    grad_out[...] = total

    for dz in range(1, NZ):
        zcopy(dz).wait_send()
    for slot in range(NZ):
        for dx in range(1, NX):
            xcopy(slot, dx).wait_send()
    for df in range(1, N_FEAT):
        mcopy(df).wait_send()
    for i in range(1, N_ROWS):
        ocopy(i).wait_send()
    for slot in range(NZ):
        for dx in range(NX):
            if slot != 2 or dx != 0:
                gcopy(slot, dx).wait_send()


def on_device(tile_values, tile_blocks, tile_counts, labels, owner_rank, weights):
    vmem = pl.BlockSpec(memory_space=pltpu.VMEM)
    dma = pltpu.SemaphoreType.DMA
    own, grad, loss = pl.pallas_call(
        body,
        out_shape=(
            jax.ShapeDtypeStruct((2, 128), F32),
            jax.ShapeDtypeStruct((32, 128), F32),
            jax.ShapeDtypeStruct((1, 128), F32),
        ),
        in_specs=[pl.BlockSpec(memory_space=pl.ANY)] + [vmem] * 5,
        out_specs=(vmem, vmem, vmem),
        scratch_shapes=[
            pltpu.VMEM((256, 64, 128), BF),
            pltpu.VMEM((16384, 256), BF),
            pltpu.VMEM((16384, 512), BF),
            pltpu.VMEM((PAIRS, 2, 8, 128), F32),
            pltpu.VMEM((NZ, NX, 32, 128), BF),
            pltpu.VMEM((2, 256, 256), BF),
            pltpu.VMEM((PAIRS, PAIRS), I32),
            pltpu.VMEM((PAIRS, PAIRS), I32),
            pltpu.VMEM((PAIRS, PAIRS), F32),
            pltpu.VMEM((256, 128), BF),
            pltpu.VMEM((N_FEAT, 2, 128), F32),
            pltpu.VMEM((N_ROWS, 1, 128), F32),
            pltpu.VMEM((N_ROWS, 1, 128), F32),
            pltpu.VMEM((N_ROWS, 128), F32),
            pltpu.VMEM((256, 256), F32),
            pltpu.VMEM((NZ, NX, 32, 128), BF),
            pltpu.VMEM((NZ, NX, 32, 128), BF),
            dma((VCHUNKS,)),
            dma((NZ - 1,)), dma((NZ - 1,)),
            dma((NZ, NX - 1)), dma((NZ, NX - 1)),
            dma((N_FEAT - 1,)), dma((N_FEAT - 1,)),
            dma((N_ROWS - 1,)), dma((N_ROWS - 1,)),
            dma((NZ, NX)), dma((NZ, NX)),
        ],
        compiler_params=pltpu.CompilerParams(
            collective_id=0, has_side_effects=True, vmem_limit_bytes=56 * 1024 * 1024),
    )(tile_values, tile_blocks, tile_counts, labels.reshape(2, 128), owner_rank.reshape(2, 128), weights)
    return own.reshape(256), grad, loss[0, 0]


def solution(mesh):
    in_specs = (
        P("rows", "feat", None),
        P("rows", "feat"),
        P("rows", "feat"),
        P("rows"),
        P("rows"),
        P(("feat", "rows"), None),
    )
    out_specs = (P("rows"), P(("feat", "rows"), None), P())
    return jax.shard_map(
        on_device, mesh=mesh, in_specs=in_specs, out_specs=out_specs, check_vma=False
    )
```

time: 196 us -> 58.7 us (0.30); the launches traced: 193 us -> 58.4 us
  local copies, waits for them, and re-layouts: 67.5 us -> 5.61 us
  Pallas kernels: 0 us -> 50.4 us
  matrix products: 47.7 us -> 0 us
  starting transfers between devices: 35.7 us -> 0 us
  waiting for transfers between devices: 26.1 us -> 0 us
  other arithmetic: 13.6 us -> 0 us
    gather x2 -> x0, local copies, waits for them, and re-layouts: 59.3 us -> none  [the longest x1 57.4 us: on_device(): picked = weight_table[tile_blocks]]
    pallas_call x0 -> x1, Pallas kernels: none -> 50.4 us  [on_device(): pl.pallas_call(body, out_shape=(jax.ShapeDtypeStruct((2, 128), F32), jax....]
    dot_general x16 -> x0, matrix products: 47.7 us -> none  [add_block(): lax.dot_general(spread, block_values, (((0,), (0,)), ((), ())), preferred...]
    all_to_all x5 -> x0, starting transfers between devices: 35.7 us -> none  [the longest x3 22.6 us: sent_to_all(): lax.all_to_all(jnp.broadcast_to(value[None], (peers, *value.shape)), axis...]
    all_to_all x5 -> x0, waiting for transfers between devices: 26.1 us -> none  [the longest x3 14.7 us: sent_to_all(): lax.all_to_all(jnp.broadcast_to(value[None], (peers, *value.shape)), axis...]
    reduce_sum x7 -> x0, other arithmetic: 8.63 us -> none  [the longest x1 5.74 us: on_device(): jnp.sum(tile_values.astype(jnp.float32) * picked.astype(jnp.float32), axi...]
    unnamed x8 -> x4, local copies, waits for them, and re-layouts: 0.62 us -> 5.61 us
    broadcast_in_dim x7 -> x0, local copies, waits for them, and re-layouts: 2.98 us -> none  [the longest x3 2.6 us: sent_to_all(): jnp.broadcast_to(value[None], (peers, *value.shape))]
  transfers between devices with their start and end apart: 5 -> 0, of which waited for: 4 -> 0; matrix products, arithmetic and copies ran while one was open for 31% -> 0% of each run, Pallas kernels for 0% -> 0%
where the time goes in v1:
time: 58.7 us; the launch traced here: 58.4 us
  Pallas kernels  50.4 us (86%)
  local copies, waits for them, and re-layouts  5.61 us (10%)
  between operations  2.46 us (4%)
    pallas_call x1, Pallas kernels, on_device(): pl.pallas_call(body, out_shape=(jax.ShapeDtypeStruct((2, 128), F32), jax....  50.4 us
    unnamed x4, local copies, waits for them, and re-layouts  5.61 us

profile of v1, /device:TPU:1, one launch (start us, length us, event | category | flops | bytes accessed | tf_op | source)
XLA Modules:
  0.0 58.4 jit_solution(6369930667580134264)
XLA Ops:
  0.6 1.6 %copy.9.blocks_ref = s32[256,64]{1,0:T(8,128)} copy(s32[256,64]{0,1:T(8,128)} %param.7) | data formatting | bytes 131072 | tf_op args[1]
  2.2 1.5 %copy.10.counts_ref = s32[256,1]{1,0:T(8,128)} copy(s32[256,1]{0,1:T(1,128)} %param.8) | data formatting | bytes 2048 | tf_op args[2]
  3.7 50.4 %shard_map.85 = (f32[2,128]{1,0:T(2,128)}, f32[32,128]{1,0:T(8,128)}, f32[1,128]{1,0:T(1,128)}) custom-call(bf16[256,64,128]{2,1,0:T(8,128)(2,1)} %values_hbm.1, s32[256,64]{1,0:T(8,128)} %copy.9.blocks_ref, s32[256,1]{1,0:T(8,128)} %copy.10.counts_ref, s32[2,128]{1,0:T(2,128)} %bitcast.6, s32[2,128]{1,0:T(2,128)} %bitcast.7, f32[32,128]{1,0:T(8,128)} %w_ref.1), custom_call_target="tpu_custom_call" | custom-call | tf_op jit(solution)/shard_map/pallas_call | solution.py:305
  54.1 1.2 %copy.14 = f32[256]{0:T(256)} copy(f32[256]{0:T(256)} %bitcast.5) | data formatting | bytes 2048
  55.3 1.3 %copy.15 = f32[32,128]{1,0:T(8,128)} copy(f32[32,128]{1,0:T(8,128)} %get-tuple-element.13) | data formatting | bytes 32768

commit v2 on v1

v2 whole, which is shorter than its diff:
```python
import jax
import jax.numpy as jnp
from jax import lax
from jax.experimental import pallas as pl
from jax.experimental.pallas import tpu as pltpu
from jax.sharding import PartitionSpec as P

MESH = pl.DeviceIdType.MESH
NZ, NX = 8, 4
N_ROWS = NZ * NX
N_FEAT = 8
BF = jnp.bfloat16
F32 = jnp.float32
I16 = jnp.int16
I32 = jnp.int32
PAIRS = 128
GROUP = 8
VCHUNKS = 8
FSUB = 8
BSUB = 32


def iota(shape, dim, dtype=I32):
    return lax.broadcasted_iota(I32, shape, dim).astype(dtype)


def body(
    blocks_hbm, counts_hbm, labels_hbm, owner_hbm, w_hbm, values_hbm,
    own_out, grad_out, loss_out,
    blocks_ref, counts_ref, labels_ref, owner_ref, w_ref,
    vbuf, vx, onehot, acc, wtab, cct, qrow, coef, rankhot,
    mbuf, sbuf, rbuf, xrow, gacc, gsend, grecv,
    isem, vsem, zs, zr, xs, xr, ms, mr, os_, or_, gs, gr,
):
    r = lax.axis_index("rows")
    f = lax.axis_index("feat")
    z = lax.div(r, NX)
    x = lax.rem(r, NX)

    def row_at(dz, dx):
        return lax.rem(z + dz, NZ) * NX + lax.rem(x + dx, NX)

    def feat_at(df):
        return lax.rem(f + df, N_FEAT)

    def stage_of(dz):
        return ((dz + 2) % NZ) // 4

    barrier = pltpu.get_barrier_semaphore()
    for dz in (4, 3, 5, 2, 6, 1, 7):
        pl.semaphore_signal(barrier, inc=1, device_id={"rows": row_at(dz, 0)}, device_id_type=MESH)
    for dx in (2, 1, 3):
        pl.semaphore_signal(barrier, inc=1, device_id={"rows": row_at(0, dx)}, device_id_type=MESH)
    for df in range(1, N_FEAT):
        pl.semaphore_signal(barrier, inc=1, device_id={"feat": feat_at(df)}, device_id_type=MESH)

    fetched = [
        pltpu.make_async_copy(src, dst, isem.at[i])
        for i, (src, dst) in enumerate((
            (w_hbm, w_ref), (blocks_hbm, blocks_ref), (counts_hbm, counts_ref),
            (owner_hbm, owner_ref), (labels_hbm, labels_ref)))
    ]
    for copy in fetched:
        copy.start()

    def vcopy(i):
        n = 2 * PAIRS // VCHUNKS
        part = pl.ds(i * n, n)
        return pltpu.make_async_copy(values_hbm.at[part], vbuf.at[part], vsem.at[i])

    for i in range(VCHUNKS // 2):
        vcopy(i).start()
        vcopy(i + VCHUNKS // 2).start()

    fetched[0].wait()
    wtab[0, 0, 0] = w_ref[...].astype(BF)
    pl.semaphore_wait(barrier, NZ - 1 + NX - 1 + N_FEAT - 1)

    def zcopy(dz):
        return pltpu.make_async_remote_copy(
            wtab.at[0, 0, 0], wtab.at[stage_of(dz), 0, dz % 4], zs, zr.at[dz - 1],
            device_id={"rows": row_at(NZ - dz, 0)}, device_id_type=MESH)

    def xcopy(dz, dx):
        s, q = stage_of(dz), dz % 4
        return pltpu.make_async_remote_copy(
            wtab.at[s, 0, q], wtab.at[s, dx, q], xs, xr.at[s],
            device_id={"rows": row_at(0, NX - dx)}, device_id_type=MESH)

    def all_of(ref, send_sem, recv_sem):
        return pltpu.make_async_remote_copy(
            ref, ref, send_sem, recv_sem, device_id={"rows": row_at(0, 1)}, device_id_type=MESH)

    for dz in (4, 3, 5, 2, 6, 1, 7):
        zcopy(dz).start()
    for dx in (2, 1, 3):
        xcopy(0, dx).start()

    def pass_on(*arrivals):
        for dz in arrivals:
            zcopy(dz).wait_recv()
            for dx in (2, 1, 3):
                xcopy(dz, dx).start()

    fetched[1].wait()
    fetched[2].wait()
    blocks = blocks_ref[...]
    dz = (lax.shift_right_logical(blocks, 7) - z + NZ) & (NZ - 1)
    dx = (lax.shift_right_logical(blocks, 5) - x + NX) & (NX - 1)
    stage = lax.shift_right_logical(dz + 2, 2) & 1
    code = ((lax.shift_right_logical(dz, 1) & 1) * 512 + stage * 256 + dx * 64
            + (dz & 1) * 32 + (blocks & 31))
    code = jnp.where(iota(blocks.shape, 0) < counts_ref[...], code, -1)
    cct[...] = jnp.concatenate([code[:, :PAIRS], code[:, PAIRS:]], axis=0)

    def build(i, _):
        codes = cct[...]
        for u in range(GROUP):
            k = i * GROUP + u
            wide = jnp.broadcast_to(codes[:, u:u + 1], (PAIRS, PAIRS))
            c16 = wide.astype(I16)
            q16 = (wide & 511).astype(I16)
            rows = pl.ds(pl.multiple_of(k * PAIRS, PAIRS), PAIRS)
            for t in range(4):
                hit = q16 == iota((PAIRS, PAIRS), 1, I16) + jnp.int16(128 * t)
                onehot[t, rows, :] = jnp.where(hit, jnp.ones((), BF), jnp.zeros((), BF))
            v = jnp.concatenate([vbuf[k], vbuf[k + PAIRS]], axis=0)
            zero = jnp.zeros((), BF)
            v1 = jnp.where(c16 >= jnp.int16(512), v, zero)
            vx[0, rows, :] = jnp.where(c16 >= jnp.int16(0), v - v1, zero)
            vx[1, rows, :] = v1
        cct[...] = pltpu.roll(codes, PAIRS - GROUP, 1)
        return 0

    steps = PAIRS // GROUP
    quarter = steps // 4
    for part in range(4):
        vcopy(part).wait()
        vcopy(part + VCHUNKS // 2).wait()
        lax.fori_loop(part * quarter, (part + 1) * quarter, build, 0)
        if part == 1:
            pass_on(1, 7)
        if part == 3:
            pass_on(2, 6)
    qrow[...] = (cct[...] & 511).T

    fetched[3].wait()
    fetched[4].wait()
    for h in range(2):
        mine = jnp.broadcast_to(owner_ref[pl.ds(h, 1), :], (PAIRS, PAIRS)).T
        rank = jnp.zeros((PAIRS, 1), F32)
        for g in range(2):
            same = (mine == owner_ref[pl.ds(g, 1), :]) & (
                iota((PAIRS, PAIRS), 1) + g * PAIRS < iota((PAIRS, PAIRS), 0) + h * PAIRS)
            rank = rank + jnp.sum(jnp.where(same, 1.0, 0.0), axis=1, keepdims=True)
        lane = (iota((PAIRS, PAIRS), 1) - 8 * lax.rem(r, 16)).astype(F32)
        rankhot[pl.ds(h * PAIRS, PAIRS), :] = jnp.where(rank == lane, 1.0, 0.0).astype(BF)
    pass_on(3, 5, 4)

    for s in range(2):
        all_of(wtab.at[s, pl.ds(1, NX - 1)], xs, xr.at[s]).wait_recv()
        table = jnp.concatenate(
            [wtab[s, :, pl.ds(2 * h, 2)].reshape(256, 128) for h in range(2)], axis=1)

        def forward(i, _, s=s, table=table):
            for u in range(FSUB):
                k0 = (i * FSUB + u) * GROUP
                rows = pl.ds(pl.multiple_of(k0 * PAIRS, GROUP * PAIRS), GROUP * PAIRS)
                hot = jnp.concatenate([onehot[2 * s, rows, :], onehot[2 * s + 1, rows, :]], axis=1)
                out = jnp.dot(hot, table, preferred_element_type=F32)
                prod = out[:, :128] * vx[0, rows, :].astype(F32) + out[:, 128:] * vx[1, rows, :].astype(F32)
                prod = prod.reshape(GROUP, 2, 8, 8, 128).sum(axis=2)
                for h in range(2):
                    ks = pl.ds(pl.multiple_of(k0 * 8, 8 * GROUP), 8 * GROUP)
                    part = prod[:, h].reshape(8 * GROUP, 128)
                    if s == 0:
                        acc[h, ks, :] = part
                    else:
                        acc[h, ks, :] = acc[h, ks, :] + part
            return 0

        lax.fori_loop(0, steps // FSUB, forward, 0)

    for h in range(2):
        groups = []
        for g in range(PAIRS // 8):
            total = acc[h, pl.ds(64 * g, 8, stride=8), :]
            for i in range(1, 8):
                total = total + acc[h, pl.ds(64 * g + i, 8, stride=8), :]
            groups.append(total)
        rows_sum = jnp.concatenate(groups, axis=0)
        mbuf[f, pl.ds(h, 1), :] = jnp.sum(rows_sum.T, axis=0, keepdims=True)
    for df in (4, 3, 5, 2, 6, 1, 7):
        pltpu.make_async_remote_copy(
            mbuf.at[f], mbuf.at[f], ms, mr,
            device_id={"feat": feat_at(df)}, device_id_type=MESH).start()
    all_of(mbuf.at[pl.ds(0, N_FEAT - 1)], ms, mr).wait_recv()
    margin = mbuf[0]
    for i in range(1, N_FEAT):
        margin = margin + mbuf[i]
    label = labels_ref[...].astype(F32)
    residual = 1.0 / (1.0 + jnp.exp(-margin)) - label
    resid_half = residual.astype(BF).astype(F32)
    spread = [jnp.broadcast_to(resid_half[h:h + 1, :], (PAIRS, PAIRS)).T for h in range(2)]
    coef[...] = jnp.where(iota((PAIRS, PAIRS), 1) < 64, spread[0], spread[1])

    def gradient_half(s):
        def step(i, _):
            total = None
            for t in range(BSUB):
                left = []
                for u in range(2):
                    k = (i * BSUB + t) * 2 + u
                    q16 = jnp.broadcast_to(qrow[pl.ds(k, 1), :], (16, PAIRS)).astype(I16)
                    c16 = jnp.broadcast_to(coef[pl.ds(k, 1), :], (16, PAIRS)).astype(BF)
                    q16 = jnp.concatenate([q16] * 16, axis=0)
                    c16 = jnp.concatenate([c16] * 16, axis=0)
                    hit = q16 == iota((256, PAIRS), 0, I16) + jnp.int16(256 * s)
                    left.append(jnp.where(hit, c16, jnp.zeros((), BF)))
                rows = pl.ds(pl.multiple_of((i * BSUB + t) * 2 * PAIRS, 2 * PAIRS), 2 * PAIRS)
                right = jnp.concatenate([vx[0, rows, :], vx[1, rows, :]], axis=1)
                d = jnp.dot(jnp.concatenate(left, axis=1), right, preferred_element_type=F32)
                total = d if total is None else total + d
            for h in range(2):
                gacc[h] = gacc[h] + total[:, 128 * h:128 * h + 128]
            return 0

        gacc[...] = jnp.zeros(gacc.shape, F32)
        lax.fori_loop(0, PAIRS // 2 // BSUB, step, 0)
        for h in range(2):
            for j in range(2):
                for dx in range(NX):
                    block = gacc[h, pl.ds(dx * 64 + j * 32, 32), :]
                    if s == 0 and h == 0 and j == 0 and dx == 0:
                        grad_out[...] = block
                    else:
                        gsend[s, dx * 4 + 2 * h + j] = block.astype(BF)
        for dz in ((4, 3, 5, 2) if s else (6, 7, 1, 0)):
            for dx in (2, 1, 3, 0):
                if dz != 0 or dx != 0:
                    n = dx * 4 + dz % 4
                    pltpu.make_async_remote_copy(
                        gsend.at[s, n], grecv.at[s, n], gs.at[s], gr.at[s],
                        device_id={"rows": row_at(dz, dx)}, device_id_type=MESH).start()

    gradient_half(1)

    loss_terms = jnp.maximum(margin, 0.0) + jnp.log1p(jnp.exp(-jnp.abs(margin))) - label * margin
    loss_here = jnp.sum(jnp.sum(loss_terms, axis=1, keepdims=True), axis=0, keepdims=True)
    ordered = jnp.zeros((N_ROWS, 128), F32)
    left = margin
    for _ in range(3):
        piece = left.astype(BF).astype(F32)
        left = left - piece
        pick = jnp.concatenate(
            [jnp.where(owner_ref[pl.ds(h, 1), :] == iota((N_ROWS, 128), 0), piece[h:h + 1, :], 0.0)
             for h in range(2)], axis=1).astype(BF)
        ordered = ordered + jnp.dot(pick, rankhot[...], preferred_element_type=F32)
    lane_group = lax.shift_right_logical(iota((N_ROWS, 128), 1), 3)
    xrow[...] = jnp.where(lane_group == lax.rem(r + 1, 16), loss_here, ordered)
    for d in range(N_ROWS):
        sbuf[d] = xrow[d:d + 1, :]
    rbuf[r] = xrow[pl.ds(r, 1), :]
    for i in range(1, N_ROWS):
        to = row_at(i // NX, i % NX)
        pltpu.make_async_remote_copy(
            sbuf.at[to], rbuf.at[r], os_, or_,
            device_id={"rows": to}, device_id_type=MESH).start()

    gradient_half(0)

    all_of(rbuf.at[pl.ds(0, N_ROWS - 1)], os_, or_).wait_recv()
    group1 = lax.shift_right_logical(iota((1, 128), 1), 3)
    loss_sum = jnp.zeros((1, 128), F32)
    for h in range(2):
        mine = jnp.zeros((1, 128), F32)
        for g in range(16):
            row = rbuf[h * 16 + g]
            mine = mine + jnp.where(group1 == g, row, 0.0)
            loss_sum = loss_sum + jnp.where(group1 == (g + 1) % 16, row, 0.0)
        own_out[pl.ds(h, 1), :] = mine
    loss_total = jnp.sum(loss_sum, axis=1, keepdims=True) * (1.0 / (8.0 * 8192.0))
    loss_out[...] = jnp.broadcast_to(loss_total, (1, 128))

    total = grad_out[...]
    all_of(grecv.at[1], gs.at[1], gr.at[1]).wait_recv()
    for n in range(16):
        total = total + grecv[1, n].astype(F32)
    all_of(grecv.at[0, pl.ds(1, 15)], gs.at[0], gr.at[0]).wait_recv()
    for n in range(1, 16):
        total = total + grecv[0, n].astype(F32)
    grad_out[...] = total

    all_of(gsend.at[0, pl.ds(0, NZ - 1)], zs, zr.at[0]).wait_send()
    all_of(wtab.at[pl.ds(0, 2), pl.ds(1, NX - 1)], xs, xr.at[0]).wait_send()
    all_of(mbuf.at[pl.ds(0, N_FEAT - 1)], ms, mr).wait_send()
    all_of(sbuf.at[pl.ds(0, N_ROWS - 1)], os_, or_).wait_send()
    all_of(gsend.at[1], gs.at[1], gr.at[1]).wait_send()
    all_of(gsend.at[0, pl.ds(1, 15)], gs.at[0], gr.at[0]).wait_send()


def on_device(tile_values, tile_blocks, tile_counts, labels, owner_rank, weights):
    vmem = pl.BlockSpec(memory_space=pltpu.VMEM)
    dma = pltpu.SemaphoreType.DMA
    own, grad, loss = pl.pallas_call(
        body,
        out_shape=(
            jax.ShapeDtypeStruct((2, 128), F32),
            jax.ShapeDtypeStruct((32, 128), F32),
            jax.ShapeDtypeStruct((1, 128), F32),
        ),
        in_specs=[pl.BlockSpec(memory_space=pl.ANY)] * 6,
        out_specs=(vmem, vmem, vmem),
        scratch_shapes=[
            pltpu.VMEM((64, 256), I32),
            pltpu.VMEM((1, 256), I32),
            pltpu.VMEM((2, 128), I32),
            pltpu.VMEM((2, 128), I32),
            pltpu.VMEM((32, 128), F32),
            pltpu.VMEM((256, 64, 128), BF),
            pltpu.VMEM((2, 16384, 128), BF),
            pltpu.VMEM((4, 16384, 128), BF),
            pltpu.VMEM((2, PAIRS * 8, 128), F32),
            pltpu.VMEM((2, NX, 4, 32, 128), BF),
            pltpu.VMEM((PAIRS, PAIRS), I32),
            pltpu.VMEM((PAIRS, PAIRS), I32),
            pltpu.VMEM((PAIRS, PAIRS), F32),
            pltpu.VMEM((256, 128), BF),
            pltpu.VMEM((N_FEAT, 2, 128), F32),
            pltpu.VMEM((N_ROWS, 1, 128), F32),
            pltpu.VMEM((N_ROWS, 1, 128), F32),
            pltpu.VMEM((N_ROWS, 128), F32),
            pltpu.VMEM((2, 256, 128), F32),
            pltpu.VMEM((2, 16, 32, 128), BF),
            pltpu.VMEM((2, 16, 32, 128), BF),
            dma((5,)), dma((VCHUNKS,)),
            dma, dma((NZ - 1,)),
            dma, dma((2,)),
            dma, dma,
            dma, dma,
            dma((2,)), dma((2,)),
        ],
        compiler_params=pltpu.CompilerParams(
            collective_id=0, has_side_effects=True, vmem_limit_bytes=56 * 1024 * 1024),
    )(tile_blocks.T, tile_counts.T, labels.reshape(2, 128), owner_rank.reshape(2, 128), weights, tile_values)
    return own.reshape(256), grad, loss[0, 0]


def solution(mesh):
    in_specs = (
        P("rows", "feat", None),
        P("rows", "feat"),
        P("rows", "feat"),
        P("rows"),
        P("rows"),
        P(("feat", "rows"), None),
    )
    out_specs = (P("rows"), P(("feat", "rows"), None), P())
    return jax.shard_map(
        on_device, mesh=mesh, in_specs=in_specs, out_specs=out_specs, check_vma=False
    )
```

time: 58.7 us -> 46.6 us (0.79)
  Pallas kernels: 50.4 us -> 41.3 us
  local copies, waits for them, and re-layouts: 5.61 us -> 2.54 us
    pallas_call x1, Pallas kernels: 50.4 us -> 41.3 us  [on_device(): pl.pallas_call(body, out_shape=(jax.ShapeDtypeStruct((2, 128), F32), jax....]
    unnamed x4 -> x2, local copies, waits for them, and re-layouts: 5.61 us -> 2.54 us
where the time goes in v2:
time: 46.6 us; the launch traced here: 46.3 us
  Pallas kernels  41.3 us (89%)
  local copies, waits for them, and re-layouts  2.54 us (5%)
  between operations  2.4 us (5%)
    pallas_call x1, Pallas kernels, on_device(): pl.pallas_call(body, out_shape=(jax.ShapeDtypeStruct((2, 128), F32), jax....  41.3 us
    unnamed x2, local copies, waits for them, and re-layouts  2.54 us

profile of v2, /device:TPU:1, one launch (start us, length us, event | category | flops | bytes accessed | tf_op | source)
XLA Modules:
  0.0 46.3 jit_solution(17547959131173792279)
XLA Ops:
  0.6 41.3 %shard_map.85 = (f32[2,128]{1,0:T(2,128)}, f32[32,128]{1,0:T(8,128)}, f32[1,128]{1,0:T(1,128)}) custom-call(s32[64,256]{1,0:T(8,128)} %bitcast.7, s32[1,256]{1,0:T(1,128)} %bitcast.8, s32[2,128]{1,0:T(2,128)} %bitcast.9, s32[2,128]{1,0:T(2,128)} %bitcast.10, f32[32,128]{1,0:T(8,128)} %w_hbm.1, bf16[256,64,128]{2,1,0:T(8,128)(2,1)} %values_hbm.1), custom_call_target="tpu_custom_call" | custom-call | tf_op jit(solution)/shard_map/pallas_call | solution.py:305
  42.0 1.2 %copy.12 = f32[256]{0:T(256)} copy(f32[256]{0:T(256)} %bitcast.11) | data formatting | bytes 2048
  43.2 1.3 %copy.13 = f32[32,128]{1,0:T(8,128)} copy(f32[32,128]{1,0:T(8,128)} %get-tuple-element.13) | data formatting | bytes 32768

commit v3 on v2

--- a/solution.py
+++ b/solution.py
@@ -17,7 +17,6 @@
 GROUP = 8
 VCHUNKS = 8
 FSUB = 8
-BSUB = 32
 
 
 def iota(shape, dim, dtype=I32):
@@ -29,7 +28,7 @@
     own_out, grad_out, loss_out,
     blocks_ref, counts_ref, labels_ref, owner_ref, w_ref,
     vbuf, vx, onehot, acc, wtab, cct, qrow, coef, rankhot,
-    mbuf, sbuf, rbuf, xrow, gacc, gsend, grecv,
+    mbuf, sbuf, rbuf, xrow, gsend, grecv,
     isem, vsem, zs, zr, xs, xr, ms, mr, os_, or_, gs, gr,
 ):
     r = lax.axis_index("rows")
@@ -43,16 +42,8 @@
     def feat_at(df):
         return lax.rem(f + df, N_FEAT)
 
-    def stage_of(dz):
-        return ((dz + 2) % NZ) // 4
-
-    barrier = pltpu.get_barrier_semaphore()
-    for dz in (4, 3, 5, 2, 6, 1, 7):
-        pl.semaphore_signal(barrier, inc=1, device_id={"rows": row_at(dz, 0)}, device_id_type=MESH)
-    for dx in (2, 1, 3):
-        pl.semaphore_signal(barrier, inc=1, device_id={"rows": row_at(0, dx)}, device_id_type=MESH)
-    for df in range(1, N_FEAT):
-        pl.semaphore_signal(barrier, inc=1, device_id={"feat": feat_at(df)}, device_id_type=MESH)
+    def place(dz):
+        return ((dz + 2) // 4) % 2, dz // 4, ((dz + 1) // 2) % 2
 
     fetched = [
         pltpu.make_async_copy(src, dst, isem.at[i])
@@ -72,35 +63,56 @@
         vcopy(i).start()
         vcopy(i + VCHUNKS // 2).start()
 
+    barrier = pltpu.get_barrier_semaphore()
+    for dz in (2, 6, 1, 7):
+        pl.semaphore_signal(barrier, inc=1, device_id={"rows": row_at(dz, 0)}, device_id_type=MESH)
+    for dx in (2, 1, 3):
+        pl.semaphore_signal(barrier, inc=1, device_id={"rows": row_at(0, dx)}, device_id_type=MESH)
+    for df in range(1, N_FEAT):
+        pl.semaphore_signal(barrier, inc=1, device_id={"feat": feat_at(df)}, device_id_type=MESH)
+
     fetched[0].wait()
-    wtab[0, 0, 0] = w_ref[...].astype(BF)
-    pl.semaphore_wait(barrier, NZ - 1 + NX - 1 + N_FEAT - 1)
+    wtab[0, 0, 0, 0] = w_ref[...].astype(BF)
+    pl.semaphore_wait(barrier, 4 + NX - 1 + N_FEAT - 1)
+
+    def slot(dz, dx):
+        return wtab.at[(*place(dz), dx)]
 
     def zcopy(dz):
         return pltpu.make_async_remote_copy(
-            wtab.at[0, 0, 0], wtab.at[stage_of(dz), 0, dz % 4], zs, zr.at[dz - 1],
+            slot(0, 0), slot(dz, 0), zs, zr.at[dz],
             device_id={"rows": row_at(NZ - dz, 0)}, device_id_type=MESH)
 
-    def xcopy(dz, dx):
-        s, q = stage_of(dz), dz % 4
+    def xcopy(dz, dx, recv_sem):
         return pltpu.make_async_remote_copy(
-            wtab.at[s, 0, q], wtab.at[s, dx, q], xs, xr.at[s],
+            slot(dz, 0), slot(dz, dx), xs, recv_sem,
             device_id={"rows": row_at(0, NX - dx)}, device_id_type=MESH)
+
+    def relay(dz, step, dx):
+        return pltpu.make_async_remote_copy(
+            slot(dz, 0), slot(dz + step, dx), xs, xr.at[1],
+            device_id={"rows": row_at(NZ - step, NX - dx)}, device_id_type=MESH)
 
     def all_of(ref, send_sem, recv_sem):
         return pltpu.make_async_remote_copy(
             ref, ref, send_sem, recv_sem, device_id={"rows": row_at(0, 1)}, device_id_type=MESH)
 
-    for dz in (4, 3, 5, 2, 6, 1, 7):
+    for dz in (2, 6, 1, 7):
         zcopy(dz).start()
     for dx in (2, 1, 3):
-        xcopy(0, dx).start()
-
-    def pass_on(*arrivals):
-        for dz in arrivals:
+        xcopy(0, dx, xr.at[2]).start()
+
+    def pass_on():
+        for dz in (1, 7, 2, 6):
             zcopy(dz).wait_recv()
             for dx in (2, 1, 3):
-                xcopy(dz, dx).start()
+                xcopy(dz, dx, xr.at[place(dz)[0]]).start()
+        all_of(gsend.at[0, pl.ds(0, 3)], xs, xr.at[2]).wait_recv()
+        for dx in (2, 1, 3, 0):
+            relay(2, 2, dx).start()
+        for dx in (2, 1, 3, 0):
+            relay(2, 1, dx).start()
+            relay(6, -1, dx).start()
 
     fetched[1].wait()
     fetched[2].wait()
@@ -108,8 +120,8 @@
     dz = (lax.shift_right_logical(blocks, 7) - z + NZ) & (NZ - 1)
     dx = (lax.shift_right_logical(blocks, 5) - x + NX) & (NX - 1)
     stage = lax.shift_right_logical(dz + 2, 2) & 1
-    code = ((lax.shift_right_logical(dz, 1) & 1) * 512 + stage * 256 + dx * 64
-            + (dz & 1) * 32 + (blocks & 31))
+    piece = lax.shift_right_logical(dz + 1, 1) & 1
+    code = lax.shift_right_logical(dz, 2) * 512 + stage * 256 + piece * 128 + dx * 32 + (blocks & 31)
     code = jnp.where(iota(blocks.shape, 0) < counts_ref[...], code, -1)
     cct[...] = jnp.concatenate([code[:, :PAIRS], code[:, PAIRS:]], axis=0)
 
@@ -139,9 +151,7 @@
         vcopy(part + VCHUNKS // 2).wait()
         lax.fori_loop(part * quarter, (part + 1) * quarter, build, 0)
         if part == 1:
-            pass_on(1, 7)
-        if part == 3:
-            pass_on(2, 6)
+            pass_on()
     qrow[...] = (cct[...] & 511).T
 
     fetched[3].wait()
@@ -155,12 +165,10 @@
             rank = rank + jnp.sum(jnp.where(same, 1.0, 0.0), axis=1, keepdims=True)
         lane = (iota((PAIRS, PAIRS), 1) - 8 * lax.rem(r, 16)).astype(F32)
         rankhot[pl.ds(h * PAIRS, PAIRS), :] = jnp.where(rank == lane, 1.0, 0.0).astype(BF)
-    pass_on(3, 5, 4)
 
     for s in range(2):
-        all_of(wtab.at[s, pl.ds(1, NX - 1)], xs, xr.at[s]).wait_recv()
-        table = jnp.concatenate(
-            [wtab[s, :, pl.ds(2 * h, 2)].reshape(256, 128) for h in range(2)], axis=1)
+        all_of(gsend.at[pl.ds(0, 3), pl.ds(0, 5 if s else 3)], xs, xr.at[s]).wait_recv()
+        table = jnp.concatenate([wtab[s, h].reshape(256, 128) for h in range(2)], axis=1)
 
         def forward(i, _, s=s, table=table):
             for u in range(FSUB):
@@ -204,46 +212,41 @@
     spread = [jnp.broadcast_to(resid_half[h:h + 1, :], (PAIRS, PAIRS)).T for h in range(2)]
     coef[...] = jnp.where(iota((PAIRS, PAIRS), 1) < 64, spread[0], spread[1])
 
-    def gradient_half(s):
-        def step(i, _):
-            total = None
-            for t in range(BSUB):
-                left = []
-                for u in range(2):
-                    k = (i * BSUB + t) * 2 + u
-                    q16 = jnp.broadcast_to(qrow[pl.ds(k, 1), :], (16, PAIRS)).astype(I16)
-                    c16 = jnp.broadcast_to(coef[pl.ds(k, 1), :], (16, PAIRS)).astype(BF)
-                    q16 = jnp.concatenate([q16] * 16, axis=0)
-                    c16 = jnp.concatenate([c16] * 16, axis=0)
-                    hit = q16 == iota((256, PAIRS), 0, I16) + jnp.int16(256 * s)
-                    left.append(jnp.where(hit, c16, jnp.zeros((), BF)))
-                rows = pl.ds(pl.multiple_of((i * BSUB + t) * 2 * PAIRS, 2 * PAIRS), 2 * PAIRS)
-                right = jnp.concatenate([vx[0, rows, :], vx[1, rows, :]], axis=1)
-                d = jnp.dot(jnp.concatenate(left, axis=1), right, preferred_element_type=F32)
-                total = d if total is None else total + d
-            for h in range(2):
-                gacc[h] = gacc[h] + total[:, 128 * h:128 * h + 128]
-            return 0
-
-        gacc[...] = jnp.zeros(gacc.shape, F32)
-        lax.fori_loop(0, PAIRS // 2 // BSUB, step, 0)
+    def gradient_piece(s, j):
+        p = 2 * s + j
+        total = None
+        for t in range(PAIRS // 2):
+            left = []
+            for u in range(2):
+                k = 2 * t + u
+                q16 = jnp.broadcast_to(qrow[k:k + 1, :], (16, PAIRS)).astype(I16)
+                c16 = jnp.broadcast_to(coef[k:k + 1, :], (16, PAIRS)).astype(BF)
+                q16 = jnp.concatenate([q16] * 8, axis=0)
+                c16 = jnp.concatenate([c16] * 8, axis=0)
+                hit = q16 == iota((128, PAIRS), 0, I16) + jnp.int16(128 * p)
+                left.append(jnp.where(hit, c16, jnp.zeros((), BF)))
+            rows = pl.ds(t * 2 * PAIRS, 2 * PAIRS)
+            right = jnp.concatenate([vx[0, rows, :], vx[1, rows, :]], axis=1)
+            d = jnp.dot(jnp.concatenate(left, axis=1), right, preferred_element_type=F32)
+            total = d if total is None else total + d
         for h in range(2):
-            for j in range(2):
-                for dx in range(NX):
-                    block = gacc[h, pl.ds(dx * 64 + j * 32, 32), :]
-                    if s == 0 and h == 0 and j == 0 and dx == 0:
-                        grad_out[...] = block
-                    else:
-                        gsend[s, dx * 4 + 2 * h + j] = block.astype(BF)
-        for dz in ((4, 3, 5, 2) if s else (6, 7, 1, 0)):
-            for dx in (2, 1, 3, 0):
-                if dz != 0 or dx != 0:
-                    n = dx * 4 + dz % 4
-                    pltpu.make_async_remote_copy(
-                        gsend.at[s, n], grecv.at[s, n], gs.at[s], gr.at[s],
-                        device_id={"rows": row_at(dz, dx)}, device_id_type=MESH).start()
-
-    gradient_half(1)
+            for dx in range(NX):
+                block = total[dx * 32:dx * 32 + 32, 128 * h:128 * h + 128]
+                if p == 0 and h == 0 and dx == 0:
+                    grad_out[...] = block
+                else:
+                    gsend[p, h * 4 + dx] = block.astype(BF)
+        for dz in range(NZ):
+            if place(dz)[0] == s and place(dz)[2] == j:
+                for dx in (2, 1, 3, 0):
+                    if dz != 0 or dx != 0:
+                        n = dz // 4 * 4 + dx
+                        pltpu.make_async_remote_copy(
+                            gsend.at[p, n], grecv.at[p, n], gs.at[p], gr.at[p],
+                            device_id={"rows": row_at(dz, dx)}, device_id_type=MESH).start()
+
+    gradient_piece(1, 0)
+    gradient_piece(1, 1)
 
     loss_terms = jnp.maximum(margin, 0.0) + jnp.log1p(jnp.exp(-jnp.abs(margin))) - label * margin
     loss_here = jnp.sum(jnp.sum(loss_terms, axis=1, keepdims=True), axis=0, keepdims=True)
@@ -267,7 +270,8 @@
             sbuf.at[to], rbuf.at[r], os_, or_,
             device_id={"rows": to}, device_id_type=MESH).start()
 
-    gradient_half(0)
+    gradient_piece(0, 1)
+    gradient_piece(0, 0)
 
     all_of(rbuf.at[pl.ds(0, N_ROWS - 1)], os_, or_).wait_recv()
     group1 = lax.shift_right_logical(iota((1, 128), 1), 3)
@@ -283,32 +287,39 @@
     loss_out[...] = jnp.broadcast_to(loss_total, (1, 128))
 
     total = grad_out[...]
-    all_of(grecv.at[1], gs.at[1], gr.at[1]).wait_recv()
-    for n in range(16):
-        total = total + grecv[1, n].astype(F32)
-    all_of(grecv.at[0, pl.ds(1, 15)], gs.at[0], gr.at[0]).wait_recv()
-    for n in range(1, 16):
-        total = total + grecv[0, n].astype(F32)
+    for p in (2, 3, 1, 0):
+        first = 0 if p else 1
+        all_of(grecv.at[p, pl.ds(first, 8 - first)], gs.at[p], gr.at[p]).wait_recv()
+        for n in range(first, 8):
+            total = total + grecv[p, n].astype(F32)
     grad_out[...] = total
 
-    all_of(gsend.at[0, pl.ds(0, NZ - 1)], zs, zr.at[0]).wait_send()
-    all_of(wtab.at[pl.ds(0, 2), pl.ds(1, NX - 1)], xs, xr.at[0]).wait_send()
+    all_of(gsend.at[0, pl.ds(0, 4)], zs, zr.at[0]).wait_send()
+    all_of(vx.at[0, pl.ds(0, 27 * 32)], xs, xr.at[0]).wait_send()
     all_of(mbuf.at[pl.ds(0, N_FEAT - 1)], ms, mr).wait_send()
     all_of(sbuf.at[pl.ds(0, N_ROWS - 1)], os_, or_).wait_send()
-    all_of(gsend.at[1], gs.at[1], gr.at[1]).wait_send()
-    all_of(gsend.at[0, pl.ds(1, 15)], gs.at[0], gr.at[0]).wait_send()
+    for p in range(4):
+        first = 0 if p else 1
+        all_of(gsend.at[p, pl.ds(first, 8 - first)], gs.at[p], gr.at[p]).wait_send()
+
+
+def finish(own_in, grad_in, loss_in, own_out, grad_out, loss_out):
+    own_out[...] = own_in[...]
+    grad_out[...] = grad_in[...]
+    loss_out[...] = loss_in[...]
 
 
 def on_device(tile_values, tile_blocks, tile_counts, labels, owner_rank, weights):
     vmem = pl.BlockSpec(memory_space=pltpu.VMEM)
     dma = pltpu.SemaphoreType.DMA
-    own, grad, loss = pl.pallas_call(
+    results = (
+        jax.ShapeDtypeStruct((2, 128), F32),
+        jax.ShapeDtypeStruct((32, 128), F32),
+        jax.ShapeDtypeStruct((1, 128), F32),
+    )
+    parts = pl.pallas_call(
         body,
-        out_shape=(
-            jax.ShapeDtypeStruct((2, 128), F32),
-            jax.ShapeDtypeStruct((32, 128), F32),
-            jax.ShapeDtypeStruct((1, 128), F32),
-        ),
+        out_shape=results,
         in_specs=[pl.BlockSpec(memory_space=pl.ANY)] * 6,
         out_specs=(vmem, vmem, vmem),
         scratch_shapes=[
@@ -321,7 +332,7 @@
             pltpu.VMEM((2, 16384, 128), BF),
             pltpu.VMEM((4, 16384, 128), BF),
             pltpu.VMEM((2, PAIRS * 8, 128), F32),
-            pltpu.VMEM((2, NX, 4, 32, 128), BF),
+            pltpu.VMEM((2, 2, 2, NX, 32, 128), BF),
             pltpu.VMEM((PAIRS, PAIRS), I32),
             pltpu.VMEM((PAIRS, PAIRS), I32),
             pltpu.VMEM((PAIRS, PAIRS), F32),
@@ -330,19 +341,21 @@
             pltpu.VMEM((N_ROWS, 1, 128), F32),
             pltpu.VMEM((N_ROWS, 1, 128), F32),
             pltpu.VMEM((N_ROWS, 128), F32),
-            pltpu.VMEM((2, 256, 128), F32),
-            pltpu.VMEM((2, 16, 32, 128), BF),
-            pltpu.VMEM((2, 16, 32, 128), BF),
+            pltpu.VMEM((4, 8, 32, 128), BF),
+            pltpu.VMEM((4, 8, 32, 128), BF),
             dma((5,)), dma((VCHUNKS,)),
-            dma, dma((NZ - 1,)),
-            dma, dma((2,)),
+            dma, dma((NZ,)),
+            dma, dma((3,)),
             dma, dma,
             dma, dma,
-            dma((2,)), dma((2,)),
+            dma((4,)), dma((4,)),
         ],
         compiler_params=pltpu.CompilerParams(
             collective_id=0, has_side_effects=True, vmem_limit_bytes=56 * 1024 * 1024),
     )(tile_blocks.T, tile_counts.T, labels.reshape(2, 128), owner_rank.reshape(2, 128), weights, tile_values)
+    own, grad, loss = pl.pallas_call(
+        finish, out_shape=results, in_specs=[vmem] * 3, out_specs=(vmem, vmem, vmem),
+    )(*parts)
     return own.reshape(256), grad, loss[0, 0]
 
 

time: 46.6 us -> 41.7 us (0.89)
  local copies, waits for them, and re-layouts: 2.54 us -> 0 us
  between operations: 2.4 us -> 0.64 us
    unnamed x2 -> x0, local copies, waits for them, and re-layouts: 2.54 us -> none
    pallas_call x1 -> x2, Pallas kernels: 41.3 us -> 40.9 us  [the longest x1 39.5 us: on_device(): pl.pallas_call(body, out_shape=results, in_specs=[pl.BlockSpec(memory_spa...]
where the time goes in v3:
time: 41.7 us; the launch traced here: 41.5 us
  Pallas kernels  40.9 us (98%)
  between operations  0.64 us (2%)
    pallas_call x1, Pallas kernels, on_device(): pl.pallas_call(body, out_shape=results, in_specs=[pl.BlockSpec(memory_spa...  39.5 us
    pallas_call x1, Pallas kernels, on_device(): pl.pallas_call(finish, out_shape=results, in_specs=[vmem] * 3, out_specs=...  1.33 us

profile of v3, /device:TPU:1, one launch (start us, length us, event | category | flops | bytes accessed | tf_op | source)
XLA Modules:
  0.0 41.5 jit_solution(8060418241545813916)
XLA Ops:
  0.6 39.5 %shard_map.85 = (f32[2,128]{1,0:T(2,128)}, f32[32,128]{1,0:T(8,128)}, f32[1,128]{1,0:T(1,128)}) custom-call(s32[64,256]{1,0:T(8,128)} %bitcast.7, s32[1,256]{1,0:T(1,128)} %bitcast.8, s32[2,128]{1,0:T(2,128)} %bitcast.9, s32[2,128]{1,0:T(2,128)} %bitcast.10, f32[32,128]{1,0:T(8,128)} %w_hbm.1, bf16[256,64,128]{2,1,0:T(8,128)(2,1)} %values_hbm.1), custom_call_target="tpu_custom_call" | custom-call | tf_op jit(solution)/shard_map/pallas_call | solution.py:320
  40.2 1.3 %shard_map.86 = (f32[2,128]{1,0:T(2,128)}, f32[32,128]{1,0:T(8,128)}, f32[1,128]{1,0:T(1,128)}) custom-call(f32[2,128]{1,0:T(2,128)} %get-tuple-element.9.own_in, f32[32,128]{1,0:T(8,128)} %get-tuple-element.10.grad_in, f32[1,128]{1,0:T(1,128)} %get-tuple-element.11.loss_in), custom_call_target="tpu_custom_call" | custom-call | tf_op jit(solution)/shard_map/pallas_call | solution.py:356

commit v4 on v3

--- a/solution.py
+++ b/solution.py
@@ -212,9 +212,11 @@
     spread = [jnp.broadcast_to(resid_half[h:h + 1, :], (PAIRS, PAIRS)).T for h in range(2)]
     coef[...] = jnp.where(iota((PAIRS, PAIRS), 1) < 64, spread[0], spread[1])
 
+    one = jnp.where(r < N_ROWS, 1.0, 0.0)
+
     def gradient_piece(s, j):
         p = 2 * s + j
-        total = None
+        sums = [None, None]
         for t in range(PAIRS // 2):
             left = []
             for u in range(2):
@@ -228,7 +230,8 @@
             rows = pl.ds(t * 2 * PAIRS, 2 * PAIRS)
             right = jnp.concatenate([vx[0, rows, :], vx[1, rows, :]], axis=1)
             d = jnp.dot(jnp.concatenate(left, axis=1), right, preferred_element_type=F32)
-            total = d if total is None else total + d
+            sums[t % 2] = d if sums[t % 2] is None else sums[t % 2] + d
+        total = sums[0] + sums[1] * one
         for h in range(2):
             for dx in range(NX):
                 block = total[dx * 32:dx * 32 + 32, 128 * h:128 * h + 128]

time: 41.7 us -> 39.3 us (0.942)
  Pallas kernels: 40.9 us -> 38.5 us
    pallas_call x1, Pallas kernels: 39.5 us -> 37.2 us  [on_device(): pl.pallas_call(body, out_shape=results, in_specs=[pl.BlockSpec(memory_spa...]
where the time goes in v4:
time: 39.3 us; the launch traced here: 39.1 us
  Pallas kernels  38.5 us (98%)
  between operations  0.64 us (2%)
    pallas_call x1, Pallas kernels, on_device(): pl.pallas_call(body, out_shape=results, in_specs=[pl.BlockSpec(memory_spa...  37.2 us
    pallas_call x1, Pallas kernels, on_device(): pl.pallas_call(finish, out_shape=results, in_specs=[vmem] * 3, out_specs=...  1.33 us

profile of v4, /device:TPU:1, one launch (start us, length us, event | category | flops | bytes accessed | tf_op | source)
XLA Modules:
  0.0 39.1 jit_solution(8781391272892000191)
XLA Ops:
  0.6 37.2 %shard_map.85 = (f32[2,128]{1,0:T(2,128)}, f32[32,128]{1,0:T(8,128)}, f32[1,128]{1,0:T(1,128)}) custom-call(s32[64,256]{1,0:T(8,128)} %bitcast.7, s32[1,256]{1,0:T(1,128)} %bitcast.8, s32[2,128]{1,0:T(2,128)} %bitcast.9, s32[2,128]{1,0:T(2,128)} %bitcast.10, f32[32,128]{1,0:T(8,128)} %w_hbm.1, bf16[256,64,128]{2,1,0:T(8,128)(2,1)} %values_hbm.1), custom_call_target="tpu_custom_call" | custom-call | tf_op jit(solution)/shard_map/pallas_call | solution.py:323
  37.8 1.3 %shard_map.86 = (f32[2,128]{1,0:T(2,128)}, f32[32,128]{1,0:T(8,128)}, f32[1,128]{1,0:T(1,128)}) custom-call(f32[2,128]{1,0:T(2,128)} %get-tuple-element.9.own_in, f32[32,128]{1,0:T(8,128)} %get-tuple-element.10.grad_in, f32[1,128]{1,0:T(1,128)} %get-tuple-element.11.loss_in), custom_call_target="tpu_custom_call" | custom-call | tf_op jit(solution)/shard_map/pallas_call | solution.py:359

commit v5 on v3

--- a/solution.py
+++ b/solution.py
@@ -16,7 +16,9 @@
 PAIRS = 128
 GROUP = 8
 VCHUNKS = 8
-FSUB = 8
+LAG = 6
+ZTILE = 40
+SUMMED = (2, 3)
 
 
 def iota(shape, dim, dtype=I32):
@@ -28,8 +30,8 @@
     own_out, grad_out, loss_out,
     blocks_ref, counts_ref, labels_ref, owner_ref, w_ref,
     vbuf, vx, onehot, acc, wtab, cct, qrow, coef, rankhot,
-    mbuf, sbuf, rbuf, xrow, gsend, grecv,
-    isem, vsem, zs, zr, xs, xr, ms, mr, os_, or_, gs, gr,
+    mbuf, sbuf, rbuf, xrow, kept, gsend, grecv,
+    isem, vsem, zs, zr, xs, xr, ms, mr, os_, or_, gs, gr, fs, fr,
 ):
     r = lax.axis_index("rows")
     f = lax.axis_index("feat")
@@ -42,8 +44,9 @@
     def feat_at(df):
         return lax.rem(f + df, N_FEAT)
 
-    def place(dz):
-        return ((dz + 2) // 4) % 2, dz // 4, ((dz + 1) // 2) % 2
+    def place(dz, dx):
+        dz, dx = {(7, 2): (1, 0), (1, 0): (7, 2)}.get((dz, dx), (dz, dx))
+        return ((dz + 2) // 4) % 2, dz // 4, ((dz + 1) // 2) % 2, dx
 
     fetched = [
         pltpu.make_async_copy(src, dst, isem.at[i])
@@ -76,7 +79,7 @@
     pl.semaphore_wait(barrier, 4 + NX - 1 + N_FEAT - 1)
 
     def slot(dz, dx):
-        return wtab.at[(*place(dz), dx)]
+        return wtab.at[place(dz, dx)]
 
     def zcopy(dz):
         return pltpu.make_async_remote_copy(
@@ -102,12 +105,15 @@
     for dx in (2, 1, 3):
         xcopy(0, dx, xr.at[2]).start()
 
-    def pass_on():
-        for dz in (1, 7, 2, 6):
+    def pass_on(*arrivals):
+        for dz in arrivals:
             zcopy(dz).wait_recv()
             for dx in (2, 1, 3):
-                xcopy(dz, dx, xr.at[place(dz)[0]]).start()
-        all_of(gsend.at[0, pl.ds(0, 3)], xs, xr.at[2]).wait_recv()
+                xcopy(dz, dx, xr.at[place(dz, dx)[0]]).start()
+
+    def pass_far():
+        pass_on(2)
+        all_of(vx.at[0, pl.ds(0, 3 * 32)], xs, xr.at[2]).wait_recv()
         for dx in (2, 1, 3, 0):
             relay(2, 2, dx).start()
         for dx in (2, 1, 3, 0):
@@ -119,6 +125,10 @@
     blocks = blocks_ref[...]
     dz = (lax.shift_right_logical(blocks, 7) - z + NZ) & (NZ - 1)
     dx = (lax.shift_right_logical(blocks, 5) - x + NX) & (NX - 1)
+    peer = dz * NX + dx
+    peer = jnp.where(peer == 7 * NX + 2, NX, jnp.where(peer == NX, 7 * NX + 2, peer))
+    dz = lax.shift_right_logical(peer, 2)
+    dx = peer & (NX - 1)
     stage = lax.shift_right_logical(dz + 2, 2) & 1
     piece = lax.shift_right_logical(dz + 1, 1) & 1
     code = lax.shift_right_logical(dz, 2) * 512 + stage * 256 + piece * 128 + dx * 32 + (blocks & 31)
@@ -151,7 +161,8 @@
         vcopy(part + VCHUNKS // 2).wait()
         lax.fori_loop(part * quarter, (part + 1) * quarter, build, 0)
         if part == 1:
-            pass_on()
+            pass_on(1, 7, 6)
+            pass_far()
     qrow[...] = (cct[...] & 511).T
 
     fetched[3].wait()
@@ -167,27 +178,23 @@
         rankhot[pl.ds(h * PAIRS, PAIRS), :] = jnp.where(rank == lane, 1.0, 0.0).astype(BF)
 
     for s in range(2):
-        all_of(gsend.at[pl.ds(0, 3), pl.ds(0, 5 if s else 3)], xs, xr.at[s]).wait_recv()
+        all_of(vx.at[0, pl.ds(0, (15 if s else 9) * 32)], xs, xr.at[s]).wait_recv()
         table = jnp.concatenate([wtab[s, h].reshape(256, 128) for h in range(2)], axis=1)
 
-        def forward(i, _, s=s, table=table):
-            for u in range(FSUB):
-                k0 = (i * FSUB + u) * GROUP
-                rows = pl.ds(pl.multiple_of(k0 * PAIRS, GROUP * PAIRS), GROUP * PAIRS)
-                hot = jnp.concatenate([onehot[2 * s, rows, :], onehot[2 * s + 1, rows, :]], axis=1)
-                out = jnp.dot(hot, table, preferred_element_type=F32)
-                prod = out[:, :128] * vx[0, rows, :].astype(F32) + out[:, 128:] * vx[1, rows, :].astype(F32)
-                prod = prod.reshape(GROUP, 2, 8, 8, 128).sum(axis=2)
-                for h in range(2):
-                    ks = pl.ds(pl.multiple_of(k0 * 8, 8 * GROUP), 8 * GROUP)
-                    part = prod[:, h].reshape(8 * GROUP, 128)
-                    if s == 0:
-                        acc[h, ks, :] = part
-                    else:
-                        acc[h, ks, :] = acc[h, ks, :] + part
-            return 0
-
-        lax.fori_loop(0, steps // FSUB, forward, 0)
+        for u in range(steps):
+            k0 = u * GROUP
+            rows = pl.ds(k0 * PAIRS, GROUP * PAIRS)
+            hot = jnp.concatenate([onehot[2 * s, rows, :], onehot[2 * s + 1, rows, :]], axis=1)
+            out = jnp.dot(hot, table, preferred_element_type=F32)
+            prod = out[:, :128] * vx[0, rows, :].astype(F32) + out[:, 128:] * vx[1, rows, :].astype(F32)
+            prod = prod.reshape(GROUP, 2, 8, 8, 128).sum(axis=2)
+            for h in range(2):
+                ks = pl.ds(k0 * 8, 8 * GROUP)
+                part = prod[:, h].reshape(8 * GROUP, 128)
+                if s == 0:
+                    acc[h, ks, :] = part
+                else:
+                    acc[h, ks, :] = acc[h, ks, :] + part
 
     for h in range(2):
         groups = []
@@ -212,42 +219,6 @@
     spread = [jnp.broadcast_to(resid_half[h:h + 1, :], (PAIRS, PAIRS)).T for h in range(2)]
     coef[...] = jnp.where(iota((PAIRS, PAIRS), 1) < 64, spread[0], spread[1])
 
-    def gradient_piece(s, j):
-        p = 2 * s + j
-        total = None
-        for t in range(PAIRS // 2):
-            left = []
-            for u in range(2):
-                k = 2 * t + u
-                q16 = jnp.broadcast_to(qrow[k:k + 1, :], (16, PAIRS)).astype(I16)
-                c16 = jnp.broadcast_to(coef[k:k + 1, :], (16, PAIRS)).astype(BF)
-                q16 = jnp.concatenate([q16] * 8, axis=0)
-                c16 = jnp.concatenate([c16] * 8, axis=0)
-                hit = q16 == iota((128, PAIRS), 0, I16) + jnp.int16(128 * p)
-                left.append(jnp.where(hit, c16, jnp.zeros((), BF)))
-            rows = pl.ds(t * 2 * PAIRS, 2 * PAIRS)
-            right = jnp.concatenate([vx[0, rows, :], vx[1, rows, :]], axis=1)
-            d = jnp.dot(jnp.concatenate(left, axis=1), right, preferred_element_type=F32)
-            total = d if total is None else total + d
-        for h in range(2):
-            for dx in range(NX):
-                block = total[dx * 32:dx * 32 + 32, 128 * h:128 * h + 128]
-                if p == 0 and h == 0 and dx == 0:
-                    grad_out[...] = block
-                else:
-                    gsend[p, h * 4 + dx] = block.astype(BF)
-        for dz in range(NZ):
-            if place(dz)[0] == s and place(dz)[2] == j:
-                for dx in (2, 1, 3, 0):
-                    if dz != 0 or dx != 0:
-                        n = dz // 4 * 4 + dx
-                        pltpu.make_async_remote_copy(
-                            gsend.at[p, n], grecv.at[p, n], gs.at[p], gr.at[p],
-                            device_id={"rows": row_at(dz, dx)}, device_id_type=MESH).start()
-
-    gradient_piece(1, 0)
-    gradient_piece(1, 1)
-
     loss_terms = jnp.maximum(margin, 0.0) + jnp.log1p(jnp.exp(-jnp.abs(margin))) - label * margin
     loss_here = jnp.sum(jnp.sum(loss_terms, axis=1, keepdims=True), axis=0, keepdims=True)
     ordered = jnp.zeros((N_ROWS, 128), F32)
@@ -264,14 +235,86 @@
     for d in range(N_ROWS):
         sbuf[d] = xrow[d:d + 1, :]
     rbuf[r] = xrow[pl.ds(r, 1), :]
-    for i in range(1, N_ROWS):
-        to = row_at(i // NX, i % NX)
-        pltpu.make_async_remote_copy(
-            sbuf.at[to], rbuf.at[r], os_, or_,
-            device_id={"rows": to}, device_id_type=MESH).start()
-
-    gradient_piece(0, 1)
-    gradient_piece(0, 0)
+    def send_rows():
+        for i in range(1, N_ROWS):
+            to = row_at(i // NX, i % NX)
+            pltpu.make_async_remote_copy(
+                sbuf.at[to], rbuf.at[r], os_, or_,
+                device_id={"rows": to}, device_id_type=MESH).start()
+
+    one = jnp.where(r < N_ROWS, 1.0, 0.0)
+    sums = {p: [None, None] for p in range(4)}
+
+    def tiles(p, first, last):
+        for t in range(first, last):
+            left = []
+            for u in range(2):
+                k = 2 * t + u
+                q16 = jnp.broadcast_to(qrow[k:k + 1, :], (16, PAIRS)).astype(I16)
+                c16 = jnp.broadcast_to(coef[k:k + 1, :], (16, PAIRS)).astype(BF)
+                q16 = jnp.concatenate([q16] * 8, axis=0)
+                c16 = jnp.concatenate([c16] * 8, axis=0)
+                hit = q16 == iota((128, PAIRS), 0, I16) + jnp.int16(128 * p)
+                left.append(jnp.where(hit, c16, jnp.zeros((), BF)))
+            rows = pl.ds(t * 2 * PAIRS, 2 * PAIRS)
+            right = jnp.concatenate([vx[0, rows, :], vx[1, rows, :]], axis=1)
+            d = jnp.dot(jnp.concatenate(left, axis=1), right, preferred_element_type=F32)
+            sums[p][t % 2] = d if sums[p][t % 2] is None else sums[p][t % 2] + d
+
+    def send_piece(p):
+        total = sums[p][0] + sums[p][1] * one
+        for h in range(2):
+            for c in range(NX):
+                block = total[c * 32:c * 32 + 32, 128 * h:128 * h + 128]
+                if c == 0 and (p in SUMMED or p == 0 and h == 0):
+                    kept[p, h] = block
+                else:
+                    gsend[p, c, h] = block.astype(BF)
+        if p in SUMMED:
+            for dx in (2, 1, 3):
+                pltpu.make_async_remote_copy(
+                    gsend.at[p, dx], grecv.at[p, dx], gs.at[p], gr.at[p],
+                    device_id={"rows": row_at(0, dx)}, device_id_type=MESH).start()
+            return
+        for dx in (2, 1, 3, 0):
+            for dz in (4, 3, 5, 2, 6, 1, 7, 0):
+                s, h, j, c = place(dz, dx)
+                if 2 * s + j == p and (dz != 0 or dx != 0):
+                    pltpu.make_async_remote_copy(
+                        gsend.at[p, c, h], grecv.at[p, c, h], gs.at[p], gr.at[p],
+                        device_id={"rows": row_at(dz, dx)}, device_id_type=MESH).start()
+
+    def along_z(p):
+        all_of(gsend.at[p, pl.ds(1, NX - 1)], gs.at[p], gr.at[p]).wait_recv()
+        for h in range(2):
+            block = kept[p, h]
+            for dx in range(1, NX):
+                block = block + grecv[p, dx, h].astype(F32)
+            gsend[p, 0, h] = block.astype(BF)
+        for dz in (4, 3, 5, 2):
+            s, h, j, _ = place(dz, 0)
+            if 2 * s + j == p:
+                pltpu.make_async_remote_copy(
+                    gsend.at[p, 0, h], grecv.at[p, 0, h], fs, fr,
+                    device_id={"rows": row_at(dz, 0)}, device_id_type=MESH).start()
+
+    count = PAIRS // 2
+    tiles(2, 0, count)
+    tiles(3, 0, LAG)
+    send_piece(2)
+    tiles(3, LAG, count)
+    tiles(1, 0, LAG)
+    send_piece(3)
+    send_rows()
+    tiles(1, LAG, count)
+    tiles(0, 0, LAG)
+    send_piece(1)
+    tiles(0, LAG, ZTILE)
+    along_z(2)
+    tiles(0, ZTILE, count)
+    send_piece(0)
+    if 3 in SUMMED:
+        along_z(3)
 
     all_of(rbuf.at[pl.ds(0, N_ROWS - 1)], os_, or_).wait_recv()
     group1 = lax.shift_right_logical(iota((1, 128), 1), 3)
@@ -286,21 +329,28 @@
     loss_total = jnp.sum(loss_sum, axis=1, keepdims=True) * (1.0 / (8.0 * 8192.0))
     loss_out[...] = jnp.broadcast_to(loss_total, (1, 128))
 
-    total = grad_out[...]
-    for p in (2, 3, 1, 0):
+    total = kept[0, 0]
+    for p in (3, 1, 2, 0):
+        if p in SUMMED:
+            continue
         first = 0 if p else 1
-        all_of(grecv.at[p, pl.ds(first, 8 - first)], gs.at[p], gr.at[p]).wait_recv()
+        all_of(vx.at[0, pl.ds(0, (8 - first) * 32)], gs.at[p], gr.at[p]).wait_recv()
         for n in range(first, 8):
-            total = total + grecv[p, n].astype(F32)
+            total = total + grecv[p, n // 2, n % 2].astype(F32)
+    all_of(vx.at[0, pl.ds(0, 2 * len(SUMMED) * 32)], fs, fr).wait_recv()
+    for p in SUMMED:
+        for h in range(2):
+            total = total + grecv[p, 0, h].astype(F32)
     grad_out[...] = total
 
-    all_of(gsend.at[0, pl.ds(0, 4)], zs, zr.at[0]).wait_send()
+    all_of(vx.at[0, pl.ds(0, 4 * 32)], zs, zr.at[0]).wait_send()
     all_of(vx.at[0, pl.ds(0, 27 * 32)], xs, xr.at[0]).wait_send()
     all_of(mbuf.at[pl.ds(0, N_FEAT - 1)], ms, mr).wait_send()
     all_of(sbuf.at[pl.ds(0, N_ROWS - 1)], os_, or_).wait_send()
     for p in range(4):
-        first = 0 if p else 1
-        all_of(gsend.at[p, pl.ds(first, 8 - first)], gs.at[p], gr.at[p]).wait_send()
+        sent = 6 if p in SUMMED else 8 if p else 7
+        all_of(vx.at[0, pl.ds(0, sent * 32)], gs.at[p], gr.at[p]).wait_send()
+    all_of(vx.at[0, pl.ds(0, 2 * len(SUMMED) * 32)], fs, fr).wait_send()
 
 
 def finish(own_in, grad_in, loss_in, own_out, grad_out, loss_out):
@@ -341,20 +391,23 @@
             pltpu.VMEM((N_ROWS, 1, 128), F32),
             pltpu.VMEM((N_ROWS, 1, 128), F32),
             pltpu.VMEM((N_ROWS, 128), F32),
-            pltpu.VMEM((4, 8, 32, 128), BF),
-            pltpu.VMEM((4, 8, 32, 128), BF),
+            pltpu.VMEM((4, 2, 32, 128), F32),
+            pltpu.VMEM((4, NX, 2, 32, 128), BF),
+            pltpu.VMEM((4, NX, 2, 32, 128), BF),
             dma((5,)), dma((VCHUNKS,)),
             dma, dma((NZ,)),
             dma, dma((3,)),
             dma, dma,
             dma, dma,
             dma((4,)), dma((4,)),
+            dma, dma,
         ],
         compiler_params=pltpu.CompilerParams(
-            collective_id=0, has_side_effects=True, vmem_limit_bytes=56 * 1024 * 1024),
-    )(tile_blocks.T, tile_counts.T, labels.reshape(2, 128), owner_rank.reshape(2, 128), weights, tile_values)
+            collective_id=0, has_side_effects=True, vmem_limit_bytes=40 * 1024 * 1024),
+    )(*[pltpu.with_memory_space_constraint(a, pltpu.HBM) for a in (tile_blocks.T, tile_counts.T, labels.reshape(2, 128), owner_rank.reshape(2, 128), weights, tile_values)])
     own, grad, loss = pl.pallas_call(
         finish, out_shape=results, in_specs=[vmem] * 3, out_specs=(vmem, vmem, vmem),
+        compiler_params=pltpu.CompilerParams(vmem_limit_bytes=1024 * 1024),
     )(*parts)
     return own.reshape(256), grad, loss[0, 0]
 

time: 41.7 us -> 36.3 us (0.87)
  Pallas kernels: 40.9 us -> 35.6 us
    pallas_call x1, Pallas kernels: 39.5 us -> 34.9 us  [on_device(): pl.pallas_call(body, out_shape=results, in_specs=[pl.BlockSpec(memory_spa...]
    pallas_call x1, Pallas kernels: 1.33 us -> 0.61 us  [on_device(): pl.pallas_call(finish, out_shape=results, in_specs=[vmem] * 3, out_specs=...]
where the time goes in v5:
time: 36.3 us; the launch traced here: 36.2 us
  Pallas kernels  35.6 us (98%)
  between operations  0.64 us (2%)
    pallas_call x1, Pallas kernels, on_device(): pl.pallas_call(body, out_shape=results, in_specs=[pl.BlockSpec(memory_spa...  34.9 us

profile of v5, /device:TPU:1, one launch (start us, length us, event | category | flops | bytes accessed | tf_op | source)
XLA Modules:
  0.0 36.2 jit_solution(15977737170033330493)
XLA Ops:
  0.6 34.9 %shard_map.85 = (f32[2,128]{1,0:T(2,128)S(1)}, f32[32,128]{1,0:T(8,128)S(1)}, f32[1,128]{1,0:T(1,128)S(1)}) custom-call(s32[64,256]{1,0:T(8,128)} %bitcast.7, s32[1,256]{1,0:T(1,128)} %bitcast.8, s32[2,128]{1,0:T(2,128)} %bitcast.9, s32[2,128]{1,0:T(2,128)} %bitcast.10, f32[32,128]{1,0:T(8,128)} %w_hbm.1, bf16[256,64,128]{2,1,0:T(8,128)(2,1)} %values_hbm.1), custom_call_target="tpu_custom_call" | custom-call | tf_op jit(solution)/shard_map/pallas_call | solution.py:370
  35.6 0.6 %shard_map.86 = (f32[2,128]{1,0:T(2,128)}, f32[32,128]{1,0:T(8,128)}, f32[1,128]{1,0:T(1,128)}) custom-call(f32[2,128]{1,0:T(2,128)S(1)} %get-tuple-element.9.own_in, f32[32,128]{1,0:T(8,128)S(1)} %get-tuple-element.10.grad_in, f32[1,128]{1,0:T(1,128)S(1)} %get-tuple-element.11.loss_in), custom_call_target="tpu_custom_call" | custom-call | tf_op jit(solution)/shard_map/pallas_call | solution.py:408

commit v6 on v5

--- a/solution.py
+++ b/solution.py
@@ -113,7 +113,7 @@
 
     def pass_far():
         pass_on(2)
-        all_of(vx.at[0, pl.ds(0, 3 * 32)], xs, xr.at[2]).wait_recv()
+        all_of(vx.at[pl.ds(0, 3 * 16)], xs, xr.at[2]).wait_recv()
         for dx in (2, 1, 3, 0):
             relay(2, 2, dx).start()
         for dx in (2, 1, 3, 0):
@@ -143,14 +143,14 @@
             c16 = wide.astype(I16)
             q16 = (wide & 511).astype(I16)
             rows = pl.ds(pl.multiple_of(k * PAIRS, PAIRS), PAIRS)
-            for t in range(4):
-                hit = q16 == iota((PAIRS, PAIRS), 1, I16) + jnp.int16(128 * t)
-                onehot[t, rows, :] = jnp.where(hit, jnp.ones((), BF), jnp.zeros((), BF))
+            for s in range(2):
+                hits = [q16 == iota((PAIRS, PAIRS), 1, I16) + jnp.int16(256 * s + 128 * t) for t in range(2)]
+                onehot[s, rows, :] = jnp.concatenate(
+                    [jnp.where(hit, jnp.ones((), BF), jnp.zeros((), BF)) for hit in hits], axis=1)
             v = jnp.concatenate([vbuf[k], vbuf[k + PAIRS]], axis=0)
             zero = jnp.zeros((), BF)
             v1 = jnp.where(c16 >= jnp.int16(512), v, zero)
-            vx[0, rows, :] = jnp.where(c16 >= jnp.int16(0), v - v1, zero)
-            vx[1, rows, :] = v1
+            vx[rows, :] = jnp.concatenate([jnp.where(c16 >= jnp.int16(0), v - v1, zero), v1], axis=1)
         cct[...] = pltpu.roll(codes, PAIRS - GROUP, 1)
         return 0
 
@@ -178,15 +178,15 @@
         rankhot[pl.ds(h * PAIRS, PAIRS), :] = jnp.where(rank == lane, 1.0, 0.0).astype(BF)
 
     for s in range(2):
-        all_of(vx.at[0, pl.ds(0, (15 if s else 9) * 32)], xs, xr.at[s]).wait_recv()
+        all_of(vx.at[pl.ds(0, (15 if s else 9) * 16)], xs, xr.at[s]).wait_recv()
         table = jnp.concatenate([wtab[s, h].reshape(256, 128) for h in range(2)], axis=1)
 
         for u in range(steps):
             k0 = u * GROUP
             rows = pl.ds(k0 * PAIRS, GROUP * PAIRS)
-            hot = jnp.concatenate([onehot[2 * s, rows, :], onehot[2 * s + 1, rows, :]], axis=1)
-            out = jnp.dot(hot, table, preferred_element_type=F32)
-            prod = out[:, :128] * vx[0, rows, :].astype(F32) + out[:, 128:] * vx[1, rows, :].astype(F32)
+            out = jnp.dot(onehot[s, rows, :], table, preferred_element_type=F32)
+            prod = out * vx[rows, :].astype(F32)
+            prod = prod[:, :128] + prod[:, 128:]
             prod = prod.reshape(GROUP, 2, 8, 8, 128).sum(axis=2)
             for h in range(2):
                 ks = pl.ds(k0 * 8, 8 * GROUP)
@@ -257,8 +257,7 @@
                 hit = q16 == iota((128, PAIRS), 0, I16) + jnp.int16(128 * p)
                 left.append(jnp.where(hit, c16, jnp.zeros((), BF)))
             rows = pl.ds(t * 2 * PAIRS, 2 * PAIRS)
-            right = jnp.concatenate([vx[0, rows, :], vx[1, rows, :]], axis=1)
-            d = jnp.dot(jnp.concatenate(left, axis=1), right, preferred_element_type=F32)
+            d = jnp.dot(jnp.concatenate(left, axis=1), vx[rows, :], preferred_element_type=F32)
             sums[p][t % 2] = d if sums[p][t % 2] is None else sums[p][t % 2] + d
 
     def send_piece(p):
@@ -334,23 +333,23 @@
         if p in SUMMED:
             continue
         first = 0 if p else 1
-        all_of(vx.at[0, pl.ds(0, (8 - first) * 32)], gs.at[p], gr.at[p]).wait_recv()
+        all_of(vx.at[pl.ds(0, (8 - first) * 16)], gs.at[p], gr.at[p]).wait_recv()
         for n in range(first, 8):
             total = total + grecv[p, n // 2, n % 2].astype(F32)
-    all_of(vx.at[0, pl.ds(0, 2 * len(SUMMED) * 32)], fs, fr).wait_recv()
+    all_of(vx.at[pl.ds(0, 2 * len(SUMMED) * 16)], fs, fr).wait_recv()
     for p in SUMMED:
         for h in range(2):
             total = total + grecv[p, 0, h].astype(F32)
     grad_out[...] = total
 
-    all_of(vx.at[0, pl.ds(0, 4 * 32)], zs, zr.at[0]).wait_send()
-    all_of(vx.at[0, pl.ds(0, 27 * 32)], xs, xr.at[0]).wait_send()
+    all_of(vx.at[pl.ds(0, 4 * 16)], zs, zr.at[0]).wait_send()
+    all_of(vx.at[pl.ds(0, 27 * 16)], xs, xr.at[0]).wait_send()
     all_of(mbuf.at[pl.ds(0, N_FEAT - 1)], ms, mr).wait_send()
     all_of(sbuf.at[pl.ds(0, N_ROWS - 1)], os_, or_).wait_send()
     for p in range(4):
         sent = 6 if p in SUMMED else 8 if p else 7
-        all_of(vx.at[0, pl.ds(0, sent * 32)], gs.at[p], gr.at[p]).wait_send()
-    all_of(vx.at[0, pl.ds(0, 2 * len(SUMMED) * 32)], fs, fr).wait_send()
+        all_of(vx.at[pl.ds(0, sent * 16)], gs.at[p], gr.at[p]).wait_send()
+    all_of(vx.at[pl.ds(0, 2 * len(SUMMED) * 16)], fs, fr).wait_send()
 
 
 def finish(own_in, grad_in, loss_in, own_out, grad_out, loss_out):
@@ -379,8 +378,8 @@
             pltpu.VMEM((2, 128), I32),
             pltpu.VMEM((32, 128), F32),
             pltpu.VMEM((256, 64, 128), BF),
-            pltpu.VMEM((2, 16384, 128), BF),
-            pltpu.VMEM((4, 16384, 128), BF),
+            pltpu.VMEM((16384, 256), BF),
+            pltpu.VMEM((2, 16384, 256), BF),
             pltpu.VMEM((2, PAIRS * 8, 128), F32),
             pltpu.VMEM((2, 2, 2, NX, 32, 128), BF),
             pltpu.VMEM((PAIRS, PAIRS), I32),

time: 36.3 us -> 35.8 us (0.986)
  Pallas kernels: 35.6 us -> 35.1 us
    pallas_call x1, Pallas kernels: 34.9 us -> 34.5 us  [on_device(): pl.pallas_call(body, out_shape=results, in_specs=[pl.BlockSpec(memory_spa...]
where the time goes in v6:
time: 35.8 us; the launch traced here: 35.7 us
  Pallas kernels  35.1 us (98%)
  between operations  0.64 us (2%)
    pallas_call x1, Pallas kernels, on_device(): pl.pallas_call(body, out_shape=results, in_specs=[pl.BlockSpec(memory_spa...  34.5 us

profile of v6, /device:TPU:1, one launch (start us, length us, event | category | flops | bytes accessed | tf_op | source)
XLA Modules:
  0.0 35.7 jit_solution(5621766321114597916)
XLA Ops:
  0.6 34.5 %shard_map.85 = (f32[2,128]{1,0:T(2,128)S(1)}, f32[32,128]{1,0:T(8,128)S(1)}, f32[1,128]{1,0:T(1,128)S(1)}) custom-call(s32[64,256]{1,0:T(8,128)} %bitcast.7, s32[1,256]{1,0:T(1,128)} %bitcast.8, s32[2,128]{1,0:T(2,128)} %bitcast.9, s32[2,128]{1,0:T(2,128)} %bitcast.10, f32[32,128]{1,0:T(8,128)} %w_hbm.1, bf16[256,64,128]{2,1,0:T(8,128)(2,1)} %values_hbm.1), custom_call_target="tpu_custom_call" | custom-call | tf_op jit(solution)/shard_map/pallas_call | solution.py:369
  35.1 0.6 %shard_map.86 = (f32[2,128]{1,0:T(2,128)}, f32[32,128]{1,0:T(8,128)}, f32[1,128]{1,0:T(1,128)}) custom-call(f32[2,128]{1,0:T(2,128)S(1)} %get-tuple-element.9.own_in, f32[32,128]{1,0:T(8,128)S(1)} %get-tuple-element.10.grad_in, f32[1,128]{1,0:T(1,128)S(1)} %get-tuple-element.11.loss_in), custom_call_target="tpu_custom_call" | custom-call | tf_op jit(solution)/shard_map/pallas_call | solution.py:407
